TPU v7x, 256 devices: a whole 4x4x8 slice. The times are simulated.
256 devices in a mesh: ens: 8 (over y, core), gx: 4 (over x), gy: 8 (over z).
Axes of the slice: x: 4, y: 4, z: 8, core: 2. Of those that a mesh axis runs over, the one named last changes fastest.
Arguments:
- log_conductivity: float32 [256, 128, 256], P(('ens', 'gx'), 'gy'), parts along dimension 0, may hold values from -3 to 3
- state: float32 [256, 128, 256], P(('ens', 'gx'), 'gy'), parts along dimension 0, may hold values from -6 to 6
- gradient: float32 [256, 128, 256], P(('ens', 'gx'), 'gy'), parts along dimension 0, may hold values from -60 to 60
- prior_sample: float32 [256, 128, 256], P(('ens', 'gx'), 'gy'), parts along dimension 0, may hold values from -6 to 6
- sensor_cells: int32 [131072], P(('ens', 'gx', 'gy')), parts along dimension 0, may hold values from 0 to 1048575, as said below
- noise_precision: float32 [131072], P(('ens', 'gx', 'gy')), parts along dimension 0, may hold values from 20 to 200
Outputs:
- step_field: float32 [256, 128, 256], P(('ens', 'gx'), 'gy'), parts along dimension 0
- residual: float32 [256, 128, 256], P(('ens', 'gx'), 'gy'), parts along dimension 0
There are 8 independent parts, one for each index of `ens`. A program takes and returns all parts, laid end to end along the dimension named above; each array names one. Nothing has to cross between parts.
Inputs may be any that keep to these rules, and one draw needn't show every extreme that they name: `sensor_cells`: sensors t * 512 to (t + 1) * 512 - 1 observe cells inside the block of cells held by the t-th device in the order gx, then gy (blocks of 8 x 16 x 256 cells); a cell may be observed by several sensors.
All inputs are finite; a program needn't handle non-finite values.
Results may differ from a plain program's by a relative error of at most 0.00015.
Values sent between devices are 32-bit elements; how exact they have to be, the bound alone decides.
A program may use at most 128 MiB of HBM per device.

v0:
```python
import jax
import jax.numpy as jnp
from jax import lax
from jax.experimental import pallas as pl
from jax.experimental.pallas import tpu as pltpu
from jax.sharding import PartitionSpec as P

MESH = pl.DeviceIdType.MESH
F32 = jnp.float32

NX, NY, NZ = 8, 16, 256
H, H1 = 4, 2
RX, RX1 = NX + 2 * H, NX // 2 + 2 * H1
ROWS = NY + 2 * H
PX, PY = 4, 8
GX, GY = NX * PX, NY * PY
REACH = 2
WIN = 2 * REACH + 1
COARSE_SWEEPS = 6
SENSORS = 512
OMEGA = 0.8
DIRS = ((1, 0), (-1, 0), (0, 1), (0, -1), (1, 1), (1, -1), (-1, 1), (-1, -1))
UNROLL = 2


def kernel(logk_ref, state_ref, grad_ref, prior_ref, cells_ref, prec_ref,
           step_ref, resid_ref,
           lk, st, pr, src, c0, z2, vl, ystage, yrecv, ystage1, yrecv1,
           kk, ca, wd, cd, sd, gg, zz, vv, cp, pp,
           c1, ca1, wd1, b1, v1, r1, p2,
           gat, chunk, cond2, ca2, wd2, rhs2, sol, weight, kc, dots, dchunk,
           h_send, h_recv, h1_send, h1_recv, g_send, g_recv, d_send, d_recv):
    px = lax.axis_index("gx")
    py = lax.axis_index("gy")
    row = lax.broadcasted_iota(jnp.int32, (ROWS, NZ), 0)
    lane = lax.broadcasted_iota(jnp.int32, (ROWS, NZ), 1)
    y_at = py * NY + jnp.where(row < NY + H, row, row - ROWS)

    def loop(low, high, body, unroll=UNROLL):
        def step(i, carry):
            body(i)
            return carry
        lax.fori_loop(low, high, step, 0, unroll=unroll)

    def exists(dx, dy):
        return (px + dx >= 0) & (px + dx < PX) & (py + dy >= 0) & (py + dy < PY)

    def halo_copy(field, ys, yr, n, h, wx, k, send, recv, reverse):
        dx, dy = DIRS[k]
        if dy == 0:
            source = field.at[h + n - wx:h + n, 0:NY] if dx == 1 else field.at[h:h + wx, 0:NY]
            target = field.at[h - wx:h, 0:NY] if dx == 1 else field.at[h + n:h + n + wx, 0:NY]
        else:
            side = 1 if dy == 1 else 0
            if dx == 0:
                source, target = ys.at[side], yr.at[side, h:h + n]
            elif dx == 1:
                source, target = ys.at[side, n - h:n], yr.at[side, 0:h]
            else:
                source, target = ys.at[side, 0:h], yr.at[side, h + n:h + n + h]
        if reverse:
            dx, dy = -dx, -dy
        return pltpu.make_async_remote_copy(
            src_ref=source, dst_ref=target, send_sem=send.at[k], recv_sem=recv.at[k],
            device_id={"gx": px + dx, "gy": py + dy}, device_id_type=MESH)

    def halo_clear(field, yr, n, h):
        @pl.when(px == 0)
        def _():
            field[0:h, 0:NY] = jnp.zeros((h, NY, NZ), F32)
            yr[:, 0:h] = jnp.zeros((2, h, H, NZ), F32)

        @pl.when(px == PX - 1)
        def _():
            field[h + n:, 0:NY] = jnp.zeros((h, NY, NZ), F32)
            yr[:, h + n:] = jnp.zeros((2, h, H, NZ), F32)

        @pl.when(py == 0)
        def _():
            yr[1] = jnp.zeros((n + 2 * h, H, NZ), F32)

        @pl.when(py == PY - 1)
        def _():
            yr[0] = jnp.zeros((n + 2 * h, H, NZ), F32)

    def put(field, ys, i, j, value):
        field[i, 0:NY] = value
        ys[0, j] = value[0:H]
        ys[1, j] = value[NY - H:NY]

    def halo_send(field, ys, yr, n, h, wx, send, recv, count=8):
        for k in range(count):
            @pl.when(exists(*DIRS[k]))
            def _(k=k):
                halo_copy(field, ys, yr, n, h, wx, k, send, recv, False).start()

    def halo_wait(field, ys, yr, n, h, wx, send, recv, count=8):
        for k in range(count):
            @pl.when(exists(-DIRS[k][0], -DIRS[k][1]))
            def _(k=k):
                halo_copy(field, ys, yr, n, h, wx, k, send, recv, True).wait_recv()

        def place(i):
            field[i, NY:ROWS] = jnp.concatenate([yr[0, i], yr[1, i]], axis=0)
        loop(0, n + 2 * h, place, 4)

    def halo_done(field, ys, yr, n, h, wx, send, recv, count=8):
        for k in range(count):
            @pl.when(exists(*DIRS[k]))
            def _(k=k):
                halo_copy(field, ys, yr, n, h, wx, k, send, recv, False).wait_send()

    def fine(field, slot, wx):
        return (field, ystage.at[slot], yrecv.at[slot], NX, H, wx, h_send.at[slot], h_recv.at[slot])

    def coarse(slot):
        return (vl.at[slot], ystage1.at[slot], yrecv1.at[slot], NX // 2, H1, H1, h1_send.at[slot], h1_recv.at[slot])

    PEERS = [(dx, dy) for dy in (0, 1, -1, 2, -2) for dx in (1, 3, 2, 0) if (dx, dy) != (0, 0)]

    def gather_copy(g, dx, dy):
        return pltpu.make_async_remote_copy(
            src_ref=chunk.at[g], dst_ref=gat.at[g, REACH - dy, px],
            send_sem=g_send.at[g, REACH - dy, dx], recv_sem=g_recv.at[g, REACH - dy, px],
            device_id={"gx": lax.rem(px + dx, PX), "gy": py + dy}, device_id_type=MESH)

    def gather_arrival(g, dx, dy):
        from_x = lax.rem(px + dx, PX)
        return pltpu.make_async_remote_copy(
            src_ref=chunk.at[g], dst_ref=gat.at[g, REACH + dy, from_x],
            send_sem=g_send.at[g, REACH - dy, dx], recv_sem=g_recv.at[g, REACH + dy, from_x],
            device_id={"gx": from_x, "gy": py + dy}, device_id_type=MESH)

    def gather_send(g):
        for dx, dy in PEERS:
            @pl.when((py + dy >= 0) & (py + dy < PY))
            def _(dx=dx, dy=dy):
                gather_copy(g, dx, dy).start()
        gat[g, REACH, px] = chunk[g]

    def gather_wait(g, out):
        for dx, dy in PEERS:
            @pl.when((py + dy >= 0) & (py + dy < PY))
            def _(dx=dx, dy=dy):
                gather_arrival(g, dx, dy).wait_recv()
        for d in range(WIN):
            valid = (py - REACH + d >= 0) & (py - REACH + d < PY)
            whole = jnp.concatenate([gat[g, d, p] for p in range(PX)], axis=0)
            out[d] = jnp.where(valid, whole, 0.0)

    def gather_done(g):
        for dx, dy in PEERS:
            @pl.when((py + dy >= 0) & (py + dy < PY))
            def _(dx=dx, dy=dy):
                gather_copy(g, dx, dy).wait_send()

    OTHERS = [(dx, dy) for dy in range(PY) for dx in range(PX) if (dx, dy) != (0, 0)]

    def dot_copy(g, dx, dy, arrival):
        to_x, to_y = lax.rem(px + dx, PX), lax.rem(py + dy, PY)
        slot = to_x * PY + to_y if arrival else px * PY + py
        return pltpu.make_async_remote_copy(
            src_ref=dchunk.at[g], dst_ref=dots.at[g, slot],
            send_sem=d_send.at[g, dx * PY + dy], recv_sem=d_recv.at[g, slot],
            device_id={"gx": to_x, "gy": to_y}, device_id_type=MESH)

    def dot_send(g, values):
        folded = [jnp.sum(v[:, 0:NZ // 2] + v[:, NZ // 2:NZ], axis=0, keepdims=True) for v in values]
        part = jnp.concatenate(folded, axis=0)
        dchunk[g] = part
        for dx, dy in OTHERS:
            dot_copy(g, dx, dy, False).start()
        dots[g, px * PY + py] = part

    def dot_wait(g):
        for dx, dy in OTHERS:
            dot_copy(g, dx, dy, True).wait_recv()
        total = dots[g, 0]
        for slot in range(1, PX * PY):
            total = total + dots[g, slot]
        for dx, dy in OTHERS:
            dot_copy(g, dx, dy, False).wait_send()
        return [jnp.sum(total[i:i + 1], axis=1, keepdims=True) for i in range(total.shape[0])]

    def beside(field, i, value, s):
        return (field[i - 1], field[i + 1], pltpu.roll(value, s, 0), pltpu.roll(value, ROWS - s, 0),
                pltpu.roll(value, s, 1), pltpu.roll(value, NZ - s, 1))

    def coupled(coefs, field, i, value, s):
        near = beside(field, i, value, s)
        total = coefs[0, i] * near[0]
        for f in range(1, 6):
            total = total + coefs[f, i] * near[f]
        return total

    def swap(value, s, axis):
        index, size = (row, ROWS) if axis == 0 else (lane, NZ)
        return jnp.where((index & s) == 0, pltpu.roll(value, size - s, axis), pltpu.roll(value, s, axis))

    def block_sum(low, high, s):
        total = low + high
        total = total + swap(total, s, 1)
        return total + swap(total, s, 0)

    def pick_chunk(value):
        mine = ((row & 3) == 0) & ((row >> 2) == (lane & 3)) & (row < NY)
        return jnp.sum(jnp.where(mine, value, 0.0), axis=0, keepdims=True)

    def inside_yz(s):
        return (y_at >= s, y_at < GY - s, lane >= s, lane < NZ - s)

    def cell_inside(x):
        return jnp.where((x >= 0) & (x < PX * NX), ((y_at >= 0) & (y_at < GY)).astype(F32), 0.0) > 0.5

    barrier = pltpu.get_barrier_semaphore()
    fields = [(lk, 0), (st, 1), (pr, 2), (src, 3), (z2.at[0], 4), (c0, 5), (z2.at[1], 6)]
    for field, slot in fields:
        halo_clear(field, yrecv.at[slot], NX, H)
    for slot in range(4):
        halo_clear(vl.at[slot], yrecv1.at[slot], NX // 2, H1)
    for dx, dy in OTHERS:
        pl.semaphore_signal(barrier, inc=1, device_id={"gx": lax.rem(px + dx, PX), "gy": lax.rem(py + dy, PY)},
                            device_id_type=MESH)

    def bring(i):
        put(pr, ystage.at[2], i + H, i, prior_ref[i])
        put(lk, ystage.at[0], i + H, i, logk_ref[i])
        put(st, ystage.at[1], i + H, i, state_ref[i])
    loop(0, NX, bring)
    pl.semaphore_wait(barrier, len(OTHERS))

    send_prior, send_lk, send_st = fine(pr, 2, 1), fine(lk, 0, H), fine(st, 1, H)
    halo_send(*send_prior, count=4)
    halo_send(*send_lk)
    halo_send(*send_st)

    cells = cells_ref[...]
    at_xy = ((cells >> 15) - px * NX) * NY + ((cells >> 8) & (GY - 1)) - py * NY
    at_z = cells & (NZ - 1)
    hot_xy = lax.broadcasted_iota(jnp.int32, (NX * NY, SENSORS), 0) == at_xy
    hot_z = (lax.broadcasted_iota(jnp.int32, (NZ, SENSORS), 0) == at_z).astype(F32).astype(jnp.bfloat16)
    left = jnp.where(hot_xy, prec_ref[...], 0.0)
    total = jnp.zeros((NX * NY, NZ), F32)
    for part in range(3):
        piece = left.astype(jnp.bfloat16)
        left = left - piece.astype(F32)
        total = total + lax.dot_general(piece, hot_z, (((1,), (1,)), ((), ())), preferred_element_type=F32)
    for i in range(NX):
        weight[i] = total[i * NY:(i + 1) * NY]

    halo_wait(*send_prior, count=4)

    def start_source(i):
        value = pr[i + H]
        near = beside(pr, i + H, value, 1)
        away = near[0] + near[1] + near[2] + near[3]
        away = away + jnp.where(lane >= 1, near[4], 0.0) + jnp.where(lane < NZ - 1, near[5], 0.0)
        own = (6.5 * value - away)[0:NY] - grad_ref[i]
        put(src, ystage.at[3], i + H, i, own)
    loop(0, NX, start_source)
    send_src = fine(src, 3, H)
    halo_send(*send_src)

    halo_wait(*send_lk)

    def start_cond(i):
        kk[i] = jnp.exp(lk[i])
    loop(0, RX, start_cond)

    inner = inside_yz(1)

    def start_couplings(i):
        value = kk[i]
        x = px * NX + i - H
        near = beside(kk, i, value, 1)
        in_x = (x > 0, x < GX - 1)
        diag = None
        for f in range(6):
            ok = in_x[f] if f < 2 else inner[f - 2]
            a = 0.5 * (value + jnp.where(ok, near[f], value))
            ca[f, i] = jnp.where(ok, a, 0.0)
            diag = a if diag is None else diag + a
        wd[i] = jnp.where(cell_inside(x), OMEGA / diag, 0.0)
    loop(1, RX - 1, start_couplings, 1)

    def start_level1(i):
        c1[i] = block_sum(kk[2 * i], kk[2 * i + 1], 1) * 0.125
    loop(0, RX1, start_level1)

    for i in range(2):
        chunk[0, i:i + 1] = pick_chunk(block_sum(c1[H1 + 2 * i], c1[H1 + 2 * i + 1], 2) * 0.125)
    gather_send(0)

    inner1 = inside_yz(2)

    def start_couplings1(i):
        value = c1[i]
        x = px * NX + 2 * i - H
        near = beside(c1, i, value, 2)
        in_x = (x > 0, x < GX - 2)
        diag = None
        for f in range(6):
            ok = in_x[f] if f < 2 else inner1[f - 2]
            a = value + jnp.where(ok, near[f], value)
            ca1[f, i] = jnp.where(ok, a, 0.0)
            diag = a if diag is None else diag + a
        wd1[i] = jnp.where(cell_inside(x), OMEGA / diag, 0.0)
    loop(1, RX1 - 1, start_couplings1, 1)

    halo_wait(*send_st)

    def start_state(i):
        value = st[i]
        x = px * NX + i - H
        near = beside(st, i, value, 1)
        in_x = (x > 0, x < GX - 1)
        diag = None
        for f in range(6):
            ok = in_x[f] if f < 2 else inner[f - 2]
            d = jnp.where(ok, 0.5 * (value - near[f]), value)
            cd[f, i] = jnp.where(ok, d, 0.0)
            diag = d if diag is None else diag + d
        sd[i] = diag
    loop(1, RX - 1, start_state, 1)

    row8 = lax.broadcasted_iota(jnp.int32, (8, NZ), 0)
    lane8 = lax.broadcasted_iota(jnp.int32, (8, NZ), 1)
    y_in = lane8 & 3

    def coarse_beside(values, d):
        v = values[d]
        zero = jnp.zeros_like(v)
        low = values[d - 1] if d > 0 else zero
        high = values[d + 1] if d < WIN - 1 else zero
        return (pltpu.roll(v, 1, 0), pltpu.roll(v, 7, 0),
                jnp.where(y_in > 0, pltpu.roll(v, 1, 1), pltpu.roll(low, NZ - 3, 1)),
                jnp.where(y_in < 3, pltpu.roll(v, NZ - 1, 1), pltpu.roll(high, 3, 1)),
                pltpu.roll(v, 4, 1), pltpu.roll(v, NZ - 4, 1))

    def coarse_couplings():
        values = [cond2[d] for d in range(WIN)]
        for d in range(WIN):
            place = py - REACH + d
            y = place * 4 + y_in
            inside = (row8 > 0, row8 < 7, y > 0, y < GY // 4 - 1, lane8 >= 4, lane8 < NZ - 4)
            diag = None
            for f, near in enumerate(coarse_beside(values, d)):
                a = 2.0 * (values[d] + jnp.where(inside[f], near, values[d]))
                ca2[f, d] = jnp.where(inside[f], a, 0.0)
                diag = a if diag is None else diag + a
            wd2[d] = jnp.where((place >= 0) & (place < PY), OMEGA / diag, 0.0)

    def coarse_solve():
        def sweep(s, values):
            out = []
            for d in range(WIN):
                total = rhs2[d]
                for f, near in enumerate(coarse_beside(values, d)):
                    total = total + ca2[f, d] * near
                out.append((1.0 - OMEGA) * values[d] + wd2[d] * total)
            return tuple(out)
        values = lax.fori_loop(1, COARSE_SWEEPS, sweep, tuple(wd2[d] * rhs2[d] for d in range(WIN)))
        for d in range(WIN):
            sol[d] = values[d]
        cell = jnp.where(row < NY, row >> 2, jnp.where(row < NY + H, 0, 3))
        for i in range(4):
            x = 2 * px - 1 + i
            at = jnp.clip(x, 0, 7)
            own, high, low = (sol[d, pl.ds(at, 1), :] for d in (REACH, REACH + 1, REACH - 1))
            spread = jnp.where(row < NY, own, jnp.where(row < NY + H, high, low))
            spread = jnp.where((lane & 3) == cell, spread, 0.0)
            spread = spread + swap(spread, 1, 1)
            spread = spread + swap(spread, 2, 1)
            p2[i] = jnp.where((x >= 0) & (x < 8), spread, 0.0)

    def solve(source, n, reach, finish, first):
        def presmooth(i):
            vv[i] = wd[i] * source[i]
        loop(1, RX - 1, presmooth)

        def restrict(i):
            parts = []
            for j in range(2):
                at = 2 * i + j
                parts.append((1.0 - OMEGA) * source[at] + coupled(ca, vv, at, vv[at], 1))
            total = block_sum(parts[0], parts[1], 1)
            b1[i] = total
            v1[i] = wd1[i] * total
        loop(1, RX1 - 1, restrict, 1)

        def level1_residual(i):
            return (1.0 - OMEGA) * b1[i] + coupled(ca1, v1, i, v1[i], 2)
        for i in range(2):
            chunk[n + 1, i:i + 1] = pick_chunk(
                block_sum(level1_residual(H1 + 2 * i), level1_residual(H1 + 2 * i + 1), 2))
        gather_send(n + 1)
        for i in range(NX // 2):
            put(vl.at[n], ystage1.at[n], H1 + i, i, v1[H1 + i, 0:NY])
        send_vl = coarse(n)
        halo_send(*send_vl)
        if first:
            gather_wait(0, cond2)
            coarse_couplings()
        gather_wait(n + 1, rhs2)
        coarse_solve()
        halo_wait(*send_vl)
        gather_done(n + 1)
        halo_done(*send_vl)

        for i in range(RX1):
            v1[i] = vl[n, i] + p2[i // 2]

        def postsmooth1(i):
            v = v1[i]
            r1[i] = (1.0 - OMEGA) * v + wd1[i] * (b1[i] + coupled(ca1, v1, i, v, 2))
        loop(1, RX1 - 1, postsmooth1)

        def correct(i):
            for j in range(2):
                vv[2 * i + j] = vv[2 * i + j] + r1[i]
        loop(1, RX1 - 1, correct)

        def postsmooth(i):
            v = vv[i]
            finish(i, (1.0 - OMEGA) * v + wd[i] * (source[i] + coupled(ca, vv, i, v, 1)))
        loop(H - reach, H + NX + reach, postsmooth)

    def hessian(r, n, keep):
        def scaled(i):
            gg[i] = kk[i] * r[i]
        loop(0, RX, scaled)

        def sensitivity(i):
            value = gg[i]
            zz[i] = sd[i] * value + coupled(cd, gg, i, value, 1)
        loop(1, RX - 1, sensitivity)

        second = z2.at[n]

        def weighted(i, value):
            put(second, ystage.at[4 + 2 * n], i, i - H, weight[i - H] * value[0:NY])
        solve(zz, 2 * n, 0, weighted, n == 0)
        send_z2 = fine(second, 4 + 2 * n, H - 1)
        halo_send(*send_z2)
        halo_wait(*send_z2)
        halo_done(*send_z2)

        def adjoint(i, value):
            pp[i] = value
        solve(second, 2 * n + 1, 1, adjoint, False)

        def assemble(i):
            p = pp[i]
            value = r[i]
            near = beside(r, i, value, 1)
            away = near[0] + near[1] + near[2] + near[3]
            away = away + jnp.where(lane >= 1, near[4], 0.0) + jnp.where(lane < NZ - 1, near[5], 0.0)
            misfit = kk[i] * (sd[i] * p - coupled(cd, pp, i, p, 1))
            keep(i, (misfit + 6.5 * value - away)[0:NY])
        loop(H, H + NX, assemble)

    halo_wait(*send_src)

    def keep_first(i, value):
        put(c0, ystage.at[5], i, i - H, value)
    hessian(src, 0, keep_first)
    send_c0 = fine(c0, 5, H)
    halo_send(*send_c0)

    def first_products(i, sums):
        r, c = src[i, 0:NY], c0[i, 0:NY]
        return sums[0] + r * r, sums[1] + r * c
    zero = jnp.zeros((NY, NZ), F32)
    both = lax.fori_loop(H, H + NX, first_products, (zero, zero))
    dot_send(0, (both[0], both[1], zero, zero))
    halo_wait(*send_c0)

    def keep_second(i, value):
        kc[i - H] = value
    hessian(c0, 1, keep_second)

    rr, rc = dot_wait(0)[:2]
    alpha = rr / rc

    def second_products(i, sums):
        r, c = src[i + H, 0:NY], c0[i + H, 0:NY]
        later = r - alpha * c
        curved = c - alpha * kc[i]
        return (sums[0] + later * later, sums[1] + later * curved, sums[2] + later * c, sums[3] + r * curved)
    four = lax.fori_loop(0, NX, second_products, (zero, zero, zero, zero))
    dot_send(1, four)
    norm, product, cross, crossed = dot_wait(1)
    ratio = norm / rr
    beta = norm / (product + ratio * (cross + crossed) + ratio * ratio * rc)

    def finish(i):
        r, c = src[i + H, 0:NY], c0[i + H, 0:NY]
        later = r - alpha * c
        curved = c - alpha * kc[i]
        step_ref[i] = alpha * r + beta * (later + ratio * r)
        resid_ref[i] = later - beta * (curved + ratio * c)
    loop(0, NX, finish)

    halo_done(*send_prior, count=4)
    for done in (send_lk, send_st, send_src, send_c0):
        halo_done(*done)
    gather_done(0)


def scratch():
    vmem = lambda *shape: pltpu.VMEM(shape, F32)
    fine = lambda *lead: vmem(*lead, RX, ROWS, NZ)
    level1 = lambda *lead: vmem(*lead, RX1, ROWS, NZ)
    dma = pltpu.SemaphoreType.DMA
    return [
        fine(), fine(), fine(), fine(), fine(), fine(2), level1(4),
        vmem(7, 2, NX, H, NZ), vmem(7, 2, RX, H, NZ), vmem(4, 2, NX // 2, H, NZ), vmem(4, 2, RX1, H, NZ),
        fine(), fine(6), fine(), fine(6), fine(), fine(), fine(), fine(), vmem(1, 8, 128), fine(),
        level1(), level1(6), level1(), level1(), level1(), level1(), vmem(4, ROWS, NZ),
        vmem(5, WIN, PX, 2, NZ), vmem(5, 2, NZ), vmem(WIN, 8, NZ), vmem(6, WIN, 8, NZ), vmem(WIN, 8, NZ),
        vmem(WIN, 8, NZ), vmem(WIN, 8, NZ), vmem(NX, NY, NZ), vmem(NX, NY, NZ),
        vmem(2, PX * PY, 4, 128), vmem(2, 4, 128),
        dma((7, 8)), dma((7, 8)), dma((4, 8)), dma((4, 8)), dma((5, WIN, PX)), dma((5, WIN, PX)),
        dma((2, PX * PY)), dma((2, PX * PY)),
    ]


def on_device(log_conductivity, state, gradient, prior_sample, sensor_cells, noise_precision):
    block = jax.ShapeDtypeStruct(log_conductivity.shape, F32)
    vmem = pl.BlockSpec(memory_space=pltpu.VMEM)
    return pl.pallas_call(
        kernel,
        out_shape=(block, block),
        in_specs=[vmem] * 6,
        out_specs=(vmem, vmem),
        scratch_shapes=scratch(),
        compiler_params=pltpu.CompilerParams(
            collective_id=0, has_side_effects=True, vmem_limit_bytes=60 * 1024 * 1024),
    )(log_conductivity, state, gradient, prior_sample,
      sensor_cells.reshape(1, SENSORS), noise_precision.reshape(1, SENSORS))


def solution(mesh):
    field, sensors = P(("ens", "gx"), "gy", None), P(("ens", "gx", "gy"))
    return jax.shard_map(
        on_device,
        mesh=mesh,
        in_specs=(field, field, field, field, sensors, sensors),
        out_specs=(field, field),
        check_vma=False,
    )
```

profile of v0, /device:TPU:8, one launch (start us, length us, event | category | flops | bytes accessed | tf_op | source)
XLA Modules:
  0.0 84.0 jit_solution(16019256594098691808)
XLA Ops:
  0.6 81.1 %shard_map.77 = (f32[8,16,256]{2,1,0:T(8,128)}, f32[8,16,256]{2,1,0:T(8,128)}) custom-call(f32[8,16,256]{2,1,0:T(8,128)} %logk_ref.1, f32[8,16,256]{2,1,0:T(8,128)} %state_ref.1, f32[8,16,256]{2,1,0:T(8,128)} %grad_ref.1, f32[8,16,256]{2,1,0:T(8,128)} %prior_ref.1, s32[1,512]{1,0:T(1,128)} %bitcast.2, f32[1,512]{1,0:T(1,128)} %bitcast.3), custom_call_target="tpu_custom_call" | custom-call | tf_op jit(solution)/shard_map/pallas_call | solution.py:531
  81.7 0.0 copy-start
  81.8 1.6 %copy.10 = f32[8,16,256]{2,1,0:T(8,128)} copy(f32[8,16,256]{2,1,0:T(8,128)} %get-tuple-element.4) | data formatting | bytes 262144
  83.4 0.0 copy-done
  83.4 0.7 copy.11
Async XLA Ops:
  81.7 1.6 %copy-start = (f32[8,16,256]{2,1,0:T(8,128)S(1)}, f32[8,16,256]{2,1,0:T(8,128)}, u32[]{:S(2)}) copy-start(f32[8,16,256]{2,1,0:T(8,128)} %get-tuple-element.5) | copy-start | bytes 393220
where the time goes:
time: 84.1 us; the launch traced here: 84 us
  Pallas kernels  81.1 us (96%)
  local copies, waits for them, and re-layouts  2.26 us (3%)
    pallas_call x1, Pallas kernels, on_device(): pl.pallas_call(kernel, out_shape=(block, block), in_specs=[vmem] * 6, out...  81.1 us
    unnamed x4, local copies, waits for them, and re-layouts  2.26 us

commit v1 on v0

--- a/solution.py
+++ b/solution.py
@@ -25,11 +25,11 @@
 
 def kernel(logk_ref, state_ref, grad_ref, prior_ref, cells_ref, prec_ref,
            step_ref, resid_ref,
-           lk, st, pr, src, c0, z2, vl, ystage, yrecv, ystage1, yrecv1,
+           lk, st, pr, src, c0, z2, vl, ystage, yrecv, ystage1, yrecv1, grad, cells_in, prec_in, r1f, wkeep,
            kk, ca, wd, cd, sd, gg, zz, vv, cp, pp,
            c1, ca1, wd1, b1, v1, r1, p2,
            gat, chunk, cond2, ca2, wd2, rhs2, sol, weight, kc, dots, dchunk,
-           h_send, h_recv, h1_send, h1_recv, g_send, g_recv, d_send, d_recv):
+           h_send, h_recv, h1_send, h1_recv, g_send, g_recv, d_send, d_recv, in_sem):
     px = lax.axis_index("gx")
     py = lax.axis_index("gy")
     row = lax.broadcasted_iota(jnp.int32, (ROWS, NZ), 0)
@@ -37,10 +37,16 @@
     y_at = py * NY + jnp.where(row < NY + H, row, row - ROWS)
 
     def loop(low, high, body, unroll=UNROLL):
-        def step(i, carry):
+        whole = (high - low) // unroll
+
+        def step(k, carry):
+            for j in range(unroll):
+                body(low + k * unroll + j)
+            return carry
+        if whole > 1:
+            lax.fori_loop(0, whole, step, 0)
+        for i in range(low + whole * unroll if whole > 1 else low, high):
             body(i)
-            return carry
-        lax.fori_loop(low, high, step, 0, unroll=unroll)
 
     def exists(dx, dy):
         return (px + dx >= 0) & (px + dx < PX) & (py + dy >= 0) & (py + dy < PY)
@@ -164,13 +170,15 @@
             send_sem=d_send.at[g, dx * PY + dy], recv_sem=d_recv.at[g, slot],
             device_id={"gx": to_x, "gy": to_y}, device_id_type=MESH)
 
-    def dot_send(g, values):
+    def dot_prepare(g, values):
         folded = [jnp.sum(v[:, 0:NZ // 2] + v[:, NZ // 2:NZ], axis=0, keepdims=True) for v in values]
         part = jnp.concatenate(folded, axis=0)
         dchunk[g] = part
+        dots[g, px * PY + py] = part
+
+    def dot_send(g):
         for dx, dy in OTHERS:
             dot_copy(g, dx, dy, False).start()
-        dots[g, px * PY + py] = part
 
     def dot_wait(g):
         for dx, dy in OTHERS:
@@ -193,6 +201,13 @@
             total = total + coefs[f, i] * near[f]
         return total
 
+    def prior_row(field, i):
+        value = field[i]
+        near = beside(field, i, value, 1)
+        away = near[0] + near[1] + near[2] + near[3]
+        away = away + jnp.where(lane >= 1, near[4], 0.0) + jnp.where(lane < NZ - 1, near[5], 0.0)
+        return (6.5 * value - away)[0:NY]
+
     def swap(value, s, axis):
         index, size = (row, ROWS) if axis == 0 else (lane, NZ)
         return jnp.where((index & s) == 0, pltpu.roll(value, size - s, axis), pltpu.roll(value, s, axis))
@@ -212,34 +227,51 @@
     def cell_inside(x):
         return jnp.where((x >= 0) & (x < PX * NX), ((y_at >= 0) & (y_at < GY)).astype(F32), 0.0) > 0.5
 
+    own = lambda field: field.at[H:H + NX, 0:NY]
+    loads = [pltpu.make_async_copy(source, target, in_sem.at[k]) for k, (source, target) in enumerate((
+        (prior_ref, own(pr)), (logk_ref, own(lk)), (state_ref, own(st)), (cells_ref, cells_in), (prec_ref, prec_in),
+        (grad_ref, grad)))]
+    for load in loads:
+        load.start()
     barrier = pltpu.get_barrier_semaphore()
     fields = [(lk, 0), (st, 1), (pr, 2), (src, 3), (z2.at[0], 4), (c0, 5), (z2.at[1], 6)]
     for field, slot in fields:
         halo_clear(field, yrecv.at[slot], NX, H)
     for slot in range(4):
         halo_clear(vl.at[slot], yrecv1.at[slot], NX // 2, H1)
-    for dx, dy in OTHERS:
-        pl.semaphore_signal(barrier, inc=1, device_id={"gx": lax.rem(px + dx, PX), "gy": lax.rem(py + dy, PY)},
-                            device_id_type=MESH)
-
-    def bring(i):
-        put(pr, ystage.at[2], i + H, i, prior_ref[i])
-        put(lk, ystage.at[0], i + H, i, logk_ref[i])
-        put(st, ystage.at[1], i + H, i, state_ref[i])
-    loop(0, NX, bring)
-    pl.semaphore_wait(barrier, len(OTHERS))
+    for k in range(8):
+        @pl.when(exists(*DIRS[k]))
+        def _(k=k):
+            pl.semaphore_signal(barrier, inc=1, device_id={"gx": px + DIRS[k][0], "gy": py + DIRS[k][1]},
+                                device_id_type=MESH)
+
+    def edges(field, slot):
+        for i in range(NX):
+            ystage[slot, 0, i] = field[H + i, 0:H]
+            ystage[slot, 1, i] = field[H + i, NY - H:NY]
+    loads[0].wait()
+    edges(pr, 2)
+    loads[1].wait()
+    edges(lk, 0)
+    loads[2].wait()
+    edges(st, 1)
+    across = jnp.where(px > 0, 1, 0) + jnp.where(px < PX - 1, 1, 0)
+    along = jnp.where(py > 0, 1, 0) + jnp.where(py < PY - 1, 1, 0)
+    pl.semaphore_wait(barrier, (across + 1) * (along + 1) - 1)
 
     send_prior, send_lk, send_st = fine(pr, 2, 1), fine(lk, 0, H), fine(st, 1, H)
     halo_send(*send_prior, count=4)
     halo_send(*send_lk)
     halo_send(*send_st)
 
-    cells = cells_ref[...]
+    loads[3].wait()
+    loads[4].wait()
+    cells = cells_in[...]
     at_xy = ((cells >> 15) - px * NX) * NY + ((cells >> 8) & (GY - 1)) - py * NY
     at_z = cells & (NZ - 1)
     hot_xy = lax.broadcasted_iota(jnp.int32, (NX * NY, SENSORS), 0) == at_xy
     hot_z = (lax.broadcasted_iota(jnp.int32, (NZ, SENSORS), 0) == at_z).astype(F32).astype(jnp.bfloat16)
-    left = jnp.where(hot_xy, prec_ref[...], 0.0)
+    left = jnp.where(hot_xy, prec_in[...], 0.0)
     total = jnp.zeros((NX * NY, NZ), F32)
     for part in range(3):
         piece = left.astype(jnp.bfloat16)
@@ -248,15 +280,11 @@
     for i in range(NX):
         weight[i] = total[i * NY:(i + 1) * NY]
 
+    loads[5].wait()
     halo_wait(*send_prior, count=4)
 
     def start_source(i):
-        value = pr[i + H]
-        near = beside(pr, i + H, value, 1)
-        away = near[0] + near[1] + near[2] + near[3]
-        away = away + jnp.where(lane >= 1, near[4], 0.0) + jnp.where(lane < NZ - 1, near[5], 0.0)
-        own = (6.5 * value - away)[0:NY] - grad_ref[i]
-        put(src, ystage.at[3], i + H, i, own)
+        put(src, ystage.at[3], i + H, i, prior_row(pr, i + H) - grad[i])
     loop(0, NX, start_source)
     send_src = fine(src, 3, H)
     halo_send(*send_src)
@@ -289,7 +317,6 @@
 
     for i in range(2):
         chunk[0, i:i + 1] = pick_chunk(block_sum(c1[H1 + 2 * i], c1[H1 + 2 * i + 1], 2) * 0.125)
-    gather_send(0)
 
     inner1 = inside_yz(2)
 
@@ -373,7 +400,7 @@
             spread = spread + swap(spread, 2, 1)
             p2[i] = jnp.where((x >= 0) & (x < 8), spread, 0.0)
 
-    def solve(source, n, reach, finish, first):
+    def solve(source, n, reach, finish, first, during=lambda: None, after=lambda: None):
         def presmooth(i):
             vv[i] = wd[i] * source[i]
         loop(1, RX - 1, presmooth)
@@ -401,7 +428,9 @@
         if first:
             gather_wait(0, cond2)
             coarse_couplings()
+        during()
         gather_wait(n + 1, rhs2)
+        after()
         coarse_solve()
         halo_wait(*send_vl)
         gather_done(n + 1)
@@ -425,7 +454,7 @@
             finish(i, (1.0 - OMEGA) * v + wd[i] * (source[i] + coupled(ca, vv, i, v, 1)))
         loop(H - reach, H + NX + reach, postsmooth)
 
-    def hessian(r, n, keep):
+    def hessian(r, n, keep, during, after):
         def scaled(i):
             gg[i] = kk[i] * r[i]
         loop(0, RX, scaled)
@@ -438,6 +467,7 @@
         second = z2.at[n]
 
         def weighted(i, value):
+            wkeep[n, i - H] = value[0:NY]
             put(second, ystage.at[4 + 2 * n], i, i - H, weight[i - H] * value[0:NY])
         solve(zz, 2 * n, 0, weighted, n == 0)
         send_z2 = fine(second, 4 + 2 * n, H - 1)
@@ -447,55 +477,61 @@
 
         def adjoint(i, value):
             pp[i] = value
-        solve(second, 2 * n + 1, 1, adjoint, False)
+        solve(second, 2 * n + 1, 1, adjoint, False, during, after)
 
         def assemble(i):
             p = pp[i]
-            value = r[i]
-            near = beside(r, i, value, 1)
-            away = near[0] + near[1] + near[2] + near[3]
-            away = away + jnp.where(lane >= 1, near[4], 0.0) + jnp.where(lane < NZ - 1, near[5], 0.0)
             misfit = kk[i] * (sd[i] * p - coupled(cd, pp, i, p, 1))
-            keep(i, (misfit + 6.5 * value - away)[0:NY])
+            keep(i, misfit[0:NY] + prior_row(r, i))
         loop(H, H + NX, assemble)
 
     halo_wait(*send_src)
+    gather_send(0)
+
+    zero = jnp.zeros((NY, NZ), F32)
+    sums = {}
+
+    def first_products():
+        total = [zero, zero]
+        for i in range(NX):
+            r, w = src[i + H, 0:NY], wkeep[0, i]
+            total[0] = total[0] + r * r
+            total[1] = total[1] + weight[i] * w * w + r * prior_row(src, i + H)
+        dot_prepare(0, (total[0], total[1], zero))
 
     def keep_first(i, value):
         put(c0, ystage.at[5], i, i - H, value)
-    hessian(src, 0, keep_first)
+    hessian(src, 0, keep_first, first_products, lambda: dot_send(0))
     send_c0 = fine(c0, 5, H)
     halo_send(*send_c0)
-
-    def first_products(i, sums):
-        r, c = src[i, 0:NY], c0[i, 0:NY]
-        return sums[0] + r * r, sums[1] + r * c
-    zero = jnp.zeros((NY, NZ), F32)
-    both = lax.fori_loop(H, H + NX, first_products, (zero, zero))
-    dot_send(0, (both[0], both[1], zero, zero))
     halo_wait(*send_c0)
+
+    def second_products():
+        rr, rc = dot_wait(0)[:2]
+        alpha = rr / rc
+        sums.update(rr=rr, rc=rc, alpha=alpha)
+        for i in range(H - 1, H + NX + 1):
+            r1f[i] = src[i] - alpha * c0[i]
+        total = [zero, zero, zero]
+        for i in range(NX):
+            r, w = r1f[i + H, 0:NY], wkeep[0, i] - alpha * wkeep[1, i]
+            total[0] = total[0] + r * r
+            total[1] = total[1] + weight[i] * w * w + r * prior_row(r1f, i + H)
+            total[2] = total[2] + r * c0[i + H, 0:NY]
+        dot_prepare(1, total)
+        dot_send(1)
 
     def keep_second(i, value):
         kc[i - H] = value
-    hessian(c0, 1, keep_second)
-
-    rr, rc = dot_wait(0)[:2]
-    alpha = rr / rc
-
-    def second_products(i, sums):
-        r, c = src[i + H, 0:NY], c0[i + H, 0:NY]
-        later = r - alpha * c
-        curved = c - alpha * kc[i]
-        return (sums[0] + later * later, sums[1] + later * curved, sums[2] + later * c, sums[3] + r * curved)
-    four = lax.fori_loop(0, NX, second_products, (zero, zero, zero, zero))
-    dot_send(1, four)
-    norm, product, cross, crossed = dot_wait(1)
-    ratio = norm / rr
-    beta = norm / (product + ratio * (cross + crossed) + ratio * ratio * rc)
+    hessian(c0, 1, keep_second, second_products, lambda: None)
+
+    norm, product, cross = dot_wait(1)
+    alpha = sums["alpha"]
+    ratio = norm / sums["rr"]
+    beta = norm / (product + 2.0 * ratio * cross + ratio * ratio * sums["rc"])
 
     def finish(i):
-        r, c = src[i + H, 0:NY], c0[i + H, 0:NY]
-        later = r - alpha * c
+        r, c, later = src[i + H, 0:NY], c0[i + H, 0:NY], r1f[i + H, 0:NY]
         curved = c - alpha * kc[i]
         step_ref[i] = alpha * r + beta * (later + ratio * r)
         resid_ref[i] = later - beta * (curved + ratio * c)
@@ -515,13 +551,14 @@
     return [
         fine(), fine(), fine(), fine(), fine(), fine(2), level1(4),
         vmem(7, 2, NX, H, NZ), vmem(7, 2, RX, H, NZ), vmem(4, 2, NX // 2, H, NZ), vmem(4, 2, RX1, H, NZ),
+        vmem(NX, NY, NZ), pltpu.VMEM((1, SENSORS), jnp.int32), vmem(1, SENSORS), fine(), vmem(2, NX, NY, NZ),
         fine(), fine(6), fine(), fine(6), fine(), fine(), fine(), fine(), vmem(1, 8, 128), fine(),
         level1(), level1(6), level1(), level1(), level1(), level1(), vmem(4, ROWS, NZ),
         vmem(5, WIN, PX, 2, NZ), vmem(5, 2, NZ), vmem(WIN, 8, NZ), vmem(6, WIN, 8, NZ), vmem(WIN, 8, NZ),
         vmem(WIN, 8, NZ), vmem(WIN, 8, NZ), vmem(NX, NY, NZ), vmem(NX, NY, NZ),
-        vmem(2, PX * PY, 4, 128), vmem(2, 4, 128),
+        vmem(2, PX * PY, 3, 128), vmem(2, 3, 128),
         dma((7, 8)), dma((7, 8)), dma((4, 8)), dma((4, 8)), dma((5, WIN, PX)), dma((5, WIN, PX)),
-        dma((2, PX * PY)), dma((2, PX * PY)),
+        dma((2, PX * PY)), dma((2, PX * PY)), dma((6,)),
     ]
 
 
@@ -531,13 +568,14 @@
     return pl.pallas_call(
         kernel,
         out_shape=(block, block),
-        in_specs=[vmem] * 6,
+        in_specs=[pl.BlockSpec(memory_space=pltpu.HBM)] * 6,
         out_specs=(vmem, vmem),
         scratch_shapes=scratch(),
         compiler_params=pltpu.CompilerParams(
-            collective_id=0, has_side_effects=True, vmem_limit_bytes=60 * 1024 * 1024),
-    )(log_conductivity, state, gradient, prior_sample,
-      sensor_cells.reshape(1, SENSORS), noise_precision.reshape(1, SENSORS))
+            collective_id=0, has_side_effects=True, vmem_limit_bytes=24 * 1024 * 1024),
+    )(*(pltpu.with_memory_space_constraint(x, pltpu.HBM) for x in (
+        log_conductivity, state, gradient, prior_sample,
+        sensor_cells.reshape(1, SENSORS), noise_precision.reshape(1, SENSORS))))
 
 
 def solution(mesh):

time: 84.1 us -> 72.3 us (0.86)
  Pallas kernels: 81.1 us -> 70.2 us
  local copies, waits for them, and re-layouts: 2.26 us -> 1.31 us
    pallas_call x1, Pallas kernels: 81.1 us -> 70.2 us  [on_device(): pl.pallas_call(kernel, out_shape=(block, block), in_specs=[pl.BlockSpec(m...]
    unnamed x4 -> x2, local copies, waits for them, and re-layouts: 2.26 us -> 1.31 us
where the time goes in v1:
time: 72.3 us; the launch traced here: 72.2 us
  Pallas kernels  70.2 us (97%)
  local copies, waits for them, and re-layouts  1.31 us (2%)
    pallas_call x1, Pallas kernels, on_device(): pl.pallas_call(kernel, out_shape=(block, block), in_specs=[pl.BlockSpec(m...  70.2 us

profile of v1, /device:TPU:8, one launch (start us, length us, event | category | flops | bytes accessed | tf_op | source)
XLA Modules:
  0.0 72.2 jit_solution(8715578008959613831)
XLA Ops:
  0.6 70.2 %shard_map.77 = (f32[8,16,256]{2,1,0:T(8,128)S(1)}, f32[8,16,256]{2,1,0:T(8,128)S(1)}) custom-call(f32[8,16,256]{2,1,0:T(8,128)} %logk_ref.1, f32[8,16,256]{2,1,0:T(8,128)} %state_ref.1, f32[8,16,256]{2,1,0:T(8,128)} %grad_ref.1, f32[8,16,256]{2,1,0:T(8,128)} %prior_ref.1, s32[1,512]{1,0:T(1,128)} %bitcast.2, f32[1,512]{1,0:T(1,128)} %bitcast.3), custom_call_target="tpu_custom_call" | custom-call | tf_op jit(solution)/shard_map/pallas_call | solution.py:568
  70.9 0.7 copy.10
  71.5 0.7 copy.11

commit v2 on v1

--- a/solution.py
+++ b/solution.py
@@ -17,6 +17,7 @@
 REACH = 2
 WIN = 2 * REACH + 1
 COARSE_SWEEPS = 6
+PIECES = 3
 SENSORS = 512
 OMEGA = 0.8
 DIRS = ((1, 0), (-1, 0), (0, 1), (0, -1), (1, 1), (1, -1), (-1, 1), (-1, -1))
@@ -28,12 +29,15 @@
            lk, st, pr, src, c0, z2, vl, ystage, yrecv, ystage1, yrecv1, grad, cells_in, prec_in, r1f, wkeep,
            kk, ca, wd, cd, sd, gg, zz, vv, cp, pp,
            c1, ca1, wd1, b1, v1, r1, p2,
-           gat, chunk, cond2, ca2, wd2, rhs2, sol, weight, kc, dots, dchunk,
-           h_send, h_recv, h1_send, h1_recv, g_send, g_recv, d_send, d_recv, in_sem):
+           gp, zp1, vp1, zp2, vp2, bp, v1p, gat0, gat, chunk0, chunk, cond2, ca2, wd2, rhs2, sol, weight, kc, dots, dchunk,
+           h_send, h_recv, g_send, g_recv, d_send, d_recv, in_sem):
     px = lax.axis_index("gx")
     py = lax.axis_index("gy")
     row = lax.broadcasted_iota(jnp.int32, (ROWS, NZ), 0)
     lane = lax.broadcasted_iota(jnp.int32, (ROWS, NZ), 1)
+    row8 = lax.broadcasted_iota(jnp.int32, (8, NZ), 0)
+    lane8 = lax.broadcasted_iota(jnp.int32, (8, NZ), 1)
+    y_in = lane8 & 3
     y_at = py * NY + jnp.where(row < NY + H, row, row - ROWS)
 
     def loop(low, high, body, unroll=UNROLL):
@@ -116,59 +120,71 @@
             def _(k=k):
                 halo_copy(field, ys, yr, n, h, wx, k, send, recv, False).wait_send()
 
-    def fine(field, slot, wx):
-        return (field, ystage.at[slot], yrecv.at[slot], NX, H, wx, h_send.at[slot], h_recv.at[slot])
+    def fine(field, slot, wx, sems):
+        return (field, ystage.at[slot], yrecv.at[slot], NX, H, wx, h_send.at[sems], h_recv.at[sems])
 
     def coarse(slot):
-        return (vl.at[slot], ystage1.at[slot], yrecv1.at[slot], NX // 2, H1, H1, h1_send.at[slot], h1_recv.at[slot])
+        return (vl.at[slot], ystage1.at[slot], yrecv1.at[slot], NX // 2, H1, H1, h_send.at[0], h_recv.at[0])
 
     PEERS = [(dx, dy) for dy in (0, 1, -1, 2, -2) for dx in (1, 3, 2, 0) if (dx, dy) != (0, 0)]
 
-    def gather_copy(g, dx, dy):
-        return pltpu.make_async_remote_copy(
-            src_ref=chunk.at[g], dst_ref=gat.at[g, REACH - dy, px],
-            send_sem=g_send.at[g, REACH - dy, dx], recv_sem=g_recv.at[g, REACH - dy, px],
-            device_id={"gx": lax.rem(px + dx, PX), "gy": py + dy}, device_id_type=MESH)
-
-    def gather_arrival(g, dx, dy):
-        from_x = lax.rem(px + dx, PX)
-        return pltpu.make_async_remote_copy(
-            src_ref=chunk.at[g], dst_ref=gat.at[g, REACH + dy, from_x],
-            send_sem=g_send.at[g, REACH - dy, dx], recv_sem=g_recv.at[g, REACH + dy, from_x],
-            device_id={"gx": from_x, "gy": py + dy}, device_id_type=MESH)
+    REACHED = (0, 1, -1, 2, -2)
+
+    def buffers(g):
+        return (chunk0, gat0) if g == 0 else (chunk.at[g - 1], gat.at[g - 1])
+
+    def sems(g):
+        return (g_send.at[0], g_recv.at[0]) if g == 0 else (g_send.at[1], g_recv.at[1 + (g - 1) % 2])
 
     def gather_send(g):
+        mine, all_ = buffers(g)
+        sent, arrived = sems(g)
         for dx, dy in PEERS:
             @pl.when((py + dy >= 0) & (py + dy < PY))
             def _(dx=dx, dy=dy):
-                gather_copy(g, dx, dy).start()
-        gat[g, REACH, px] = chunk[g]
-
-    def gather_wait(g, out):
-        for dx, dy in PEERS:
+                pltpu.make_async_remote_copy(
+                    src_ref=mine, dst_ref=all_.at[REACH - dy, px],
+                    send_sem=sent.at[REACH + dy], recv_sem=arrived.at[REACH - dy],
+                    device_id={"gx": lax.rem(px + dx, PX), "gy": py + dy}, device_id_type=MESH).start()
+        all_[REACH, px] = mine[...]
+
+    def gather_end(g, which):
+        all_ = buffers(g)[1]
+        for dy in REACHED:
             @pl.when((py + dy >= 0) & (py + dy < PY))
-            def _(dx=dx, dy=dy):
-                gather_arrival(g, dx, dy).wait_recv()
+            def _(dy=dy):
+                row_ = all_.at[REACH + dy, 0:PX - 1] if dy == 0 else all_.at[REACH + dy]
+                pltpu.make_async_copy(row_, row_, sems(g)[which].at[REACH + dy]).wait()
+
+    def valid(d):
+        return (py - REACH + d >= 0) & (py - REACH + d < PY)
+
+    def gather_cond():
+        gather_end(0, 1)
         for d in range(WIN):
-            valid = (py - REACH + d >= 0) & (py - REACH + d < PY)
-            whole = jnp.concatenate([gat[g, d, p] for p in range(PX)], axis=0)
-            out[d] = jnp.where(valid, whole, 0.0)
-
-    def gather_done(g):
-        for dx, dy in PEERS:
-            @pl.when((py + dy >= 0) & (py + dy < PY))
-            def _(dx=dx, dy=dy):
-                gather_copy(g, dx, dy).wait_send()
+            whole = jnp.concatenate([gat0[d, p] for p in range(PX)], axis=0)
+            cond2[d] = jnp.where(valid(d), whole, 0.0)
+
+    def along_x(piece):
+        moved = jnp.where((row8 & 1) == 0, pltpu.roll(piece, 2, 0), pltpu.roll(piece, 6, 0))
+        return jnp.where((row8 > 0) & (row8 < 7), moved, 0.0)
+
+    def gather_rhs(g):
+        gather_end(g, 1)
+        own, ring = [], []
+        for d in range(WIN):
+            piece = [jnp.concatenate([gat[g - 1, d, p, q] for p in range(PX)], axis=0) for q in range(PIECES)]
+            corner = along_x(piece[2])
+            corner = jnp.where(y_in == 0, pltpu.roll(corner, NZ - 1, 1), pltpu.roll(corner, 1, 1))
+            own.append(jnp.where(valid(d), piece[0] + along_x(piece[1]), 0.0))
+            ring.append(jnp.where(valid(d), piece[2] + corner, 0.0))
+        zero8 = jnp.zeros((8, NZ), F32)
+        for d in range(WIN):
+            low = ring[d - 1] if d > 0 else zero8
+            high = ring[d + 1] if d < WIN - 1 else zero8
+            rhs2[d] = own[d] + jnp.where(y_in == 0, low, jnp.where(y_in == 3, high, 0.0))
 
     OTHERS = [(dx, dy) for dy in range(PY) for dx in range(PX) if (dx, dy) != (0, 0)]
-
-    def dot_copy(g, dx, dy, arrival):
-        to_x, to_y = lax.rem(px + dx, PX), lax.rem(py + dy, PY)
-        slot = to_x * PY + to_y if arrival else px * PY + py
-        return pltpu.make_async_remote_copy(
-            src_ref=dchunk.at[g], dst_ref=dots.at[g, slot],
-            send_sem=d_send.at[g, dx * PY + dy], recv_sem=d_recv.at[g, slot],
-            device_id={"gx": to_x, "gy": to_y}, device_id_type=MESH)
 
     def dot_prepare(g, values):
         folded = [jnp.sum(v[:, 0:NZ // 2] + v[:, NZ // 2:NZ], axis=0, keepdims=True) for v in values]
@@ -178,16 +194,17 @@
 
     def dot_send(g):
         for dx, dy in OTHERS:
-            dot_copy(g, dx, dy, False).start()
+            pltpu.make_async_remote_copy(
+                src_ref=dchunk.at[g], dst_ref=dots.at[g, px * PY + py], send_sem=d_send.at[0], recv_sem=d_recv.at[g],
+                device_id={"gx": lax.rem(px + dx, PX), "gy": lax.rem(py + dy, PY)}, device_id_type=MESH).start()
 
     def dot_wait(g):
-        for dx, dy in OTHERS:
-            dot_copy(g, dx, dy, True).wait_recv()
+        others = dots.at[g, 0:PX * PY - 1]
+        pltpu.make_async_copy(others, others, d_recv.at[g]).wait()
         total = dots[g, 0]
         for slot in range(1, PX * PY):
             total = total + dots[g, slot]
-        for dx, dy in OTHERS:
-            dot_copy(g, dx, dy, False).wait_send()
+        pltpu.make_async_copy(others, others, d_send.at[0]).wait()
         return [jnp.sum(total[i:i + 1], axis=1, keepdims=True) for i in range(total.shape[0])]
 
     def beside(field, i, value, s):
@@ -219,6 +236,10 @@
 
     def pick_chunk(value):
         mine = ((row & 3) == 0) & ((row >> 2) == (lane & 3)) & (row < NY)
+        return jnp.sum(jnp.where(mine, value, 0.0), axis=0, keepdims=True)
+
+    def pick_ring(value, at):
+        mine = ((row == NY) & ((lane & 3) == at)) | ((row == NY + H) & ((lane & 3) == 3 - at))
         return jnp.sum(jnp.where(mine, value, 0.0), axis=0, keepdims=True)
 
     def inside_yz(s):
@@ -239,6 +260,12 @@
         halo_clear(field, yrecv.at[slot], NX, H)
     for slot in range(4):
         halo_clear(vl.at[slot], yrecv1.at[slot], NX // 2, H1)
+    for field in (gp, zp1, vp1, zp2, vp2):
+        def clear(i, field=field):
+            field[i] = jnp.zeros((ROWS, NZ), F32)
+        loop(1, RX - 1, clear)
+    for i in (0, RX1 - 1):
+        v1p[i] = jnp.zeros((ROWS, NZ), F32)
     for k in range(8):
         @pl.when(exists(*DIRS[k]))
         def _(k=k):
@@ -259,7 +286,7 @@
     along = jnp.where(py > 0, 1, 0) + jnp.where(py < PY - 1, 1, 0)
     pl.semaphore_wait(barrier, (across + 1) * (along + 1) - 1)
 
-    send_prior, send_lk, send_st = fine(pr, 2, 1), fine(lk, 0, H), fine(st, 1, H)
+    send_prior, send_lk, send_st = fine(pr, 2, 1, 0), fine(lk, 0, H, 1), fine(st, 1, H, 2)
     halo_send(*send_prior, count=4)
     halo_send(*send_lk)
     halo_send(*send_st)
@@ -285,15 +312,15 @@
 
     def start_source(i):
         put(src, ystage.at[3], i + H, i, prior_row(pr, i + H) - grad[i])
-    loop(0, NX, start_source)
-    send_src = fine(src, 3, H)
+    loop(0, NX, start_source, 8)
+    send_src = fine(src, 3, H, 3)
     halo_send(*send_src)
 
     halo_wait(*send_lk)
 
     def start_cond(i):
         kk[i] = jnp.exp(lk[i])
-    loop(0, RX, start_cond)
+    loop(0, RX, start_cond, 8)
 
     inner = inside_yz(1)
 
@@ -309,14 +336,14 @@
             ca[f, i] = jnp.where(ok, a, 0.0)
             diag = a if diag is None else diag + a
         wd[i] = jnp.where(cell_inside(x), OMEGA / diag, 0.0)
-    loop(1, RX - 1, start_couplings, 1)
+    loop(1, RX - 1, start_couplings, 14)
 
     def start_level1(i):
         c1[i] = block_sum(kk[2 * i], kk[2 * i + 1], 1) * 0.125
-    loop(0, RX1, start_level1)
+    loop(0, RX1, start_level1, 8)
 
     for i in range(2):
-        chunk[0, i:i + 1] = pick_chunk(block_sum(c1[H1 + 2 * i], c1[H1 + 2 * i + 1], 2) * 0.125)
+        chunk0[i:i + 1] = pick_chunk(block_sum(c1[H1 + 2 * i], c1[H1 + 2 * i + 1], 2) * 0.125)
 
     inner1 = inside_yz(2)
 
@@ -332,7 +359,7 @@
             ca1[f, i] = jnp.where(ok, a, 0.0)
             diag = a if diag is None else diag + a
         wd1[i] = jnp.where(cell_inside(x), OMEGA / diag, 0.0)
-    loop(1, RX1 - 1, start_couplings1, 1)
+    loop(1, RX1 - 1, start_couplings1, 6)
 
     halo_wait(*send_st)
 
@@ -348,11 +375,8 @@
             cd[f, i] = jnp.where(ok, d, 0.0)
             diag = d if diag is None else diag + d
         sd[i] = diag
-    loop(1, RX - 1, start_state, 1)
-
-    row8 = lax.broadcasted_iota(jnp.int32, (8, NZ), 0)
-    lane8 = lax.broadcasted_iota(jnp.int32, (8, NZ), 1)
-    y_in = lane8 & 3
+    loop(1, RX - 1, start_state, 14)
+
 
     def coarse_beside(values, d):
         v = values[d]
@@ -400,10 +424,34 @@
             spread = spread + swap(spread, 2, 1)
             p2[i] = jnp.where((x >= 0) & (x < 8), spread, 0.0)
 
+    def contribute(g, z, v):
+        def restrict(i):
+            parts = [(1.0 - OMEGA) * z[at] + coupled(ca, v, at, v[at], 1) for at in (2 * i, 2 * i + 1)]
+            total = block_sum(parts[0], parts[1], 1)
+            bp[i] = total
+            v1p[i] = wd1[i] * total
+        loop(1, RX1 - 1, restrict, RX1 - 2)
+
+        def level1_residual(i):
+            if i == 0:
+                return ca1[0, 1] * v1p[1]
+            if i == RX1 - 1:
+                return ca1[1, RX1 - 2] * v1p[RX1 - 2]
+            return (1.0 - OMEGA) * bp[i] + coupled(ca1, v1p, i, v1p[i], 2)
+        for j, (q, at) in enumerate(((1, 1), (0, 0), (0, 1), (1, 0))):
+            total = block_sum(level1_residual(2 * j), level1_residual(2 * j + 1), 2)
+            chunk[g - 1, q, at:at + 1] = pick_chunk(total)
+            ringed = pick_ring(total, q)
+            if q == 0:
+                chunk[g - 1, 2, at:at + 1] = ringed
+            else:
+                outer = ringed if j == 0 else jnp.concatenate([ringed, outer], axis=0)
+        chunk[g - 1, 2] = chunk[g - 1, 2] + outer
+
     def solve(source, n, reach, finish, first, during=lambda: None, after=lambda: None):
         def presmooth(i):
             vv[i] = wd[i] * source[i]
-        loop(1, RX - 1, presmooth)
+        loop(1, RX - 1, presmooth, 14)
 
         def restrict(i):
             parts = []
@@ -413,27 +461,23 @@
             total = block_sum(parts[0], parts[1], 1)
             b1[i] = total
             v1[i] = wd1[i] * total
-        loop(1, RX1 - 1, restrict, 1)
-
-        def level1_residual(i):
-            return (1.0 - OMEGA) * b1[i] + coupled(ca1, v1, i, v1[i], 2)
-        for i in range(2):
-            chunk[n + 1, i:i + 1] = pick_chunk(
-                block_sum(level1_residual(H1 + 2 * i), level1_residual(H1 + 2 * i + 1), 2))
-        gather_send(n + 1)
+        loop(1, RX1 - 1, restrict, 6)
+
         for i in range(NX // 2):
             put(vl.at[n], ystage1.at[n], H1 + i, i, v1[H1 + i, 0:NY])
         send_vl = coarse(n)
         halo_send(*send_vl)
         if first:
-            gather_wait(0, cond2)
+            gather_cond()
             coarse_couplings()
         during()
-        gather_wait(n + 1, rhs2)
+        gather_rhs(n + 1)
         after()
         coarse_solve()
         halo_wait(*send_vl)
-        gather_done(n + 1)
+        if first:
+            gather_end(0, 0)
+        gather_end(n + 1, 0)
         halo_done(*send_vl)
 
         for i in range(RX1):
@@ -442,7 +486,7 @@
         def postsmooth1(i):
             v = v1[i]
             r1[i] = (1.0 - OMEGA) * v + wd1[i] * (b1[i] + coupled(ca1, v1, i, v, 2))
-        loop(1, RX1 - 1, postsmooth1)
+        loop(1, RX1 - 1, postsmooth1, 6)
 
         def correct(i):
             for j in range(2):
@@ -452,26 +496,49 @@
         def postsmooth(i):
             v = vv[i]
             finish(i, (1.0 - OMEGA) * v + wd[i] * (source[i] + coupled(ca, vv, i, v, 1)))
-        loop(H - reach, H + NX + reach, postsmooth)
-
-    def hessian(r, n, keep, during, after):
+        loop(H - reach, H + NX + reach, postsmooth, 10)
+
+    def hessian(r, n, keep, during, after, arrive):
+        def own_scaled(i):
+            gp[i, 0:NY] = kk[i, 0:NY] * r[i, 0:NY]
+        loop(H, H + NX, own_scaled, 8)
+
+        def own_sensitivity(i):
+            value = gp[i]
+            z = sd[i] * value + coupled(cd, gp, i, value, 1)
+            zp1[i] = z
+            vp1[i] = wd[i] * z
+        loop(H - 1, H + NX + 1, own_sensitivity, 10)
+        contribute(2 * n + 1, zp1, vp1)
+        if n == 0:
+            arrive()
+            gather_send(0)
+        gather_send(2 * n + 1)
+        if n != 0:
+            arrive()
+
         def scaled(i):
             gg[i] = kk[i] * r[i]
-        loop(0, RX, scaled)
+        loop(0, RX, scaled, 8)
 
         def sensitivity(i):
             value = gg[i]
             zz[i] = sd[i] * value + coupled(cd, gg, i, value, 1)
-        loop(1, RX - 1, sensitivity)
+        loop(1, RX - 1, sensitivity, 14)
 
         second = z2.at[n]
 
         def weighted(i, value):
             wkeep[n, i - H] = value[0:NY]
-            put(second, ystage.at[4 + 2 * n], i, i - H, weight[i - H] * value[0:NY])
+            z = weight[i - H] * value[0:NY]
+            put(second, ystage.at[4 + 2 * n], i, i - H, z)
+            zp2[i, 0:NY] = z
+            vp2[i, 0:NY] = wd[i, 0:NY] * z
         solve(zz, 2 * n, 0, weighted, n == 0)
-        send_z2 = fine(second, 4 + 2 * n, H - 1)
+        send_z2 = fine(second, 4 + 2 * n, H - 1, 1)
         halo_send(*send_z2)
+        contribute(2 * n + 2, zp2, vp2)
+        gather_send(2 * n + 2)
         halo_wait(*send_z2)
         halo_done(*send_z2)
 
@@ -483,10 +550,13 @@
             p = pp[i]
             misfit = kk[i] * (sd[i] * p - coupled(cd, pp, i, p, 1))
             keep(i, misfit[0:NY] + prior_row(r, i))
-        loop(H, H + NX, assemble)
-
-    halo_wait(*send_src)
-    gather_send(0)
+        loop(H, H + NX, assemble, 8)
+
+    def arrive_first():
+        halo_wait(*send_src)
+        halo_done(*send_prior, count=4)
+        halo_done(*send_lk)
+        halo_done(*send_st)
 
     zero = jnp.zeros((NY, NZ), F32)
     sums = {}
@@ -501,10 +571,13 @@
 
     def keep_first(i, value):
         put(c0, ystage.at[5], i, i - H, value)
-    hessian(src, 0, keep_first, first_products, lambda: dot_send(0))
-    send_c0 = fine(c0, 5, H)
+    hessian(src, 0, keep_first, first_products, lambda: dot_send(0), arrive_first)
+    send_c0 = fine(c0, 5, H, 1)
     halo_send(*send_c0)
-    halo_wait(*send_c0)
+
+    def arrive_second():
+        halo_wait(*send_c0)
+        halo_done(*send_c0)
 
     def second_products():
         rr, rc = dot_wait(0)[:2]
@@ -523,7 +596,7 @@
 
     def keep_second(i, value):
         kc[i - H] = value
-    hessian(c0, 1, keep_second, second_products, lambda: None)
+    hessian(c0, 1, keep_second, second_products, lambda: None, arrive_second)
 
     norm, product, cross = dot_wait(1)
     alpha = sums["alpha"]
@@ -537,10 +610,7 @@
         resid_ref[i] = later - beta * (curved + ratio * c)
     loop(0, NX, finish)
 
-    halo_done(*send_prior, count=4)
-    for done in (send_lk, send_st, send_src, send_c0):
-        halo_done(*done)
-    gather_done(0)
+    halo_done(*send_src)
 
 
 def scratch():
@@ -554,11 +624,11 @@
         vmem(NX, NY, NZ), pltpu.VMEM((1, SENSORS), jnp.int32), vmem(1, SENSORS), fine(), vmem(2, NX, NY, NZ),
         fine(), fine(6), fine(), fine(6), fine(), fine(), fine(), fine(), vmem(1, 8, 128), fine(),
         level1(), level1(6), level1(), level1(), level1(), level1(), vmem(4, ROWS, NZ),
-        vmem(5, WIN, PX, 2, NZ), vmem(5, 2, NZ), vmem(WIN, 8, NZ), vmem(6, WIN, 8, NZ), vmem(WIN, 8, NZ),
+        fine(), fine(), fine(), fine(), fine(), level1(), level1(),
+        vmem(WIN, PX, 2, NZ), vmem(4, WIN, PX, PIECES, 2, NZ), vmem(2, NZ), vmem(4, PIECES, 2, NZ), vmem(WIN, 8, NZ), vmem(6, WIN, 8, NZ), vmem(WIN, 8, NZ),
         vmem(WIN, 8, NZ), vmem(WIN, 8, NZ), vmem(NX, NY, NZ), vmem(NX, NY, NZ),
         vmem(2, PX * PY, 3, 128), vmem(2, 3, 128),
-        dma((7, 8)), dma((7, 8)), dma((4, 8)), dma((4, 8)), dma((5, WIN, PX)), dma((5, WIN, PX)),
-        dma((2, PX * PY)), dma((2, PX * PY)), dma((6,)),
+        dma((4, 8)), dma((4, 8)), dma((2, WIN)), dma((3, WIN)), dma((1,)), dma((2,)), dma((6,)),
     ]
 
 

time: 72.3 us -> 57.8 us (0.80)
  Pallas kernels: 70.2 us -> 55.7 us
    pallas_call x1, Pallas kernels: 70.2 us -> 55.7 us  [on_device(): pl.pallas_call(kernel, out_shape=(block, block), in_specs=[pl.BlockSpec(m...]
where the time goes in v2:
time: 57.8 us; the launch traced here: 57.7 us
  Pallas kernels  55.7 us (96%)
  local copies, waits for them, and re-layouts  1.31 us (2%)
  between operations  0.64 us (1%)
    pallas_call x1, Pallas kernels, on_device(): pl.pallas_call(kernel, out_shape=(block, block), in_specs=[pl.BlockSpec(m...  55.7 us
    unnamed x2, local copies, waits for them, and re-layouts  1.31 us

profile of v2, /device:TPU:8, one launch (start us, length us, event | category | flops | bytes accessed | tf_op | source)
XLA Modules:
  0.0 57.7 jit_solution(7595918684006509296)
XLA Ops:
  0.6 55.7 %shard_map.77 = (f32[8,16,256]{2,1,0:T(8,128)S(1)}, f32[8,16,256]{2,1,0:T(8,128)S(1)}) custom-call(f32[8,16,256]{2,1,0:T(8,128)} %logk_ref.1, f32[8,16,256]{2,1,0:T(8,128)} %state_ref.1, f32[8,16,256]{2,1,0:T(8,128)} %grad_ref.1, f32[8,16,256]{2,1,0:T(8,128)} %prior_ref.1, s32[1,512]{1,0:T(1,128)} %bitcast.2, f32[1,512]{1,0:T(1,128)} %bitcast.3), custom_call_target="tpu_custom_call" | custom-call | tf_op jit(solution)/shard_map/pallas_call | solution.py:638
  56.4 0.7 %copy.10 = f32[8,16,256]{2,1,0:T(8,128)} copy(f32[8,16,256]{2,1,0:T(8,128)S(1)} %get-tuple-element.4) | data formatting | bytes 262144
  57.0 0.7 %copy.11 = f32[8,16,256]{2,1,0:T(8,128)} copy(f32[8,16,256]{2,1,0:T(8,128)S(1)} %get-tuple-element.5) | data formatting | bytes 262144

commit v3 on v2

--- a/solution.py
+++ b/solution.py
@@ -255,6 +255,11 @@
     for load in loads:
         load.start()
     barrier = pltpu.get_barrier_semaphore()
+    for k in range(8):
+        @pl.when(exists(*DIRS[k]))
+        def _(k=k):
+            pl.semaphore_signal(barrier, inc=1, device_id={"gx": px + DIRS[k][0], "gy": py + DIRS[k][1]},
+                                device_id_type=MESH)
     fields = [(lk, 0), (st, 1), (pr, 2), (src, 3), (z2.at[0], 4), (c0, 5), (z2.at[1], 6)]
     for field, slot in fields:
         halo_clear(field, yrecv.at[slot], NX, H)
@@ -266,12 +271,6 @@
         loop(1, RX - 1, clear)
     for i in (0, RX1 - 1):
         v1p[i] = jnp.zeros((ROWS, NZ), F32)
-    for k in range(8):
-        @pl.when(exists(*DIRS[k]))
-        def _(k=k):
-            pl.semaphore_signal(barrier, inc=1, device_id={"gx": px + DIRS[k][0], "gy": py + DIRS[k][1]},
-                                device_id_type=MESH)
-
     def edges(field, slot):
         for i in range(NX):
             ystage[slot, 0, i] = field[H + i, 0:H]
@@ -402,16 +401,18 @@
             wd2[d] = jnp.where((place >= 0) & (place < PY), OMEGA / diag, 0.0)
 
     def coarse_solve():
-        def sweep(s, values):
-            out = []
-            for d in range(WIN):
+        def sweep(values, low, high):
+            out = list(values)
+            for d in range(low, high):
                 total = rhs2[d]
                 for f, near in enumerate(coarse_beside(values, d)):
                     total = total + ca2[f, d] * near
-                out.append((1.0 - OMEGA) * values[d] + wd2[d] * total)
-            return tuple(out)
-        values = lax.fori_loop(1, COARSE_SWEEPS, sweep, tuple(wd2[d] * rhs2[d] for d in range(WIN)))
-        for d in range(WIN):
+                out[d] = (1.0 - OMEGA) * values[d] + wd2[d] * total
+            return out
+        values = sweep([wd2[d] * rhs2[d] for d in range(WIN)], 0, WIN)
+        for s in range(2, COARSE_SWEEPS):
+            values = sweep(values, 1, WIN - 1)
+        for d in range(1, WIN - 1):
             sol[d] = values[d]
         cell = jnp.where(row < NY, row >> 2, jnp.where(row < NY + H, 0, 3))
         for i in range(4):
@@ -424,10 +425,11 @@
             spread = spread + swap(spread, 2, 1)
             p2[i] = jnp.where((x >= 0) & (x < 8), spread, 0.0)
 
-    def contribute(g, z, v):
+    def contribute(g, z, v, out):
         def restrict(i):
-            parts = [(1.0 - OMEGA) * z[at] + coupled(ca, v, at, v[at], 1) for at in (2 * i, 2 * i + 1)]
-            total = block_sum(parts[0], parts[1], 1)
+            parts = [(1.0 - OMEGA) * z[at] + coupled(ca, v, at, v[at], 1) for at in (2 * i, 2 * i + 1)
+                     if H - out <= at < H + NX + out]
+            total = block_sum(parts[0], parts[-1] if len(parts) > 1 else 0.0, 1)
             bp[i] = total
             v1p[i] = wd1[i] * total
         loop(1, RX1 - 1, restrict, RX1 - 2)
@@ -448,7 +450,7 @@
                 outer = ringed if j == 0 else jnp.concatenate([ringed, outer], axis=0)
         chunk[g - 1, 2] = chunk[g - 1, 2] + outer
 
-    def solve(source, n, reach, finish, first, during=lambda: None, after=lambda: None):
+    def solve(source, n, reach, finish, first, after=lambda: None):
         def presmooth(i):
             vv[i] = wd[i] * source[i]
         loop(1, RX - 1, presmooth, 14)
@@ -470,7 +472,6 @@
         if first:
             gather_cond()
             coarse_couplings()
-        during()
         gather_rhs(n + 1)
         after()
         coarse_solve()
@@ -509,7 +510,7 @@
             zp1[i] = z
             vp1[i] = wd[i] * z
         loop(H - 1, H + NX + 1, own_sensitivity, 10)
-        contribute(2 * n + 1, zp1, vp1)
+        contribute(2 * n + 1, zp1, vp1, 2)
         if n == 0:
             arrive()
             gather_send(0)
@@ -537,14 +538,15 @@
         solve(zz, 2 * n, 0, weighted, n == 0)
         send_z2 = fine(second, 4 + 2 * n, H - 1, 1)
         halo_send(*send_z2)
-        contribute(2 * n + 2, zp2, vp2)
+        contribute(2 * n + 2, zp2, vp2, 1)
         gather_send(2 * n + 2)
+        during()
         halo_wait(*send_z2)
         halo_done(*send_z2)
 
         def adjoint(i, value):
             pp[i] = value
-        solve(second, 2 * n + 1, 1, adjoint, False, during, after)
+        solve(second, 2 * n + 1, 1, adjoint, False, after)
 
         def assemble(i):
             p = pp[i]

time: 57.8 us -> 53.8 us (0.931)
  Pallas kernels: 55.7 us -> 51.4 us
    pallas_call x1, Pallas kernels: 55.7 us -> 51.4 us  [on_device(): pl.pallas_call(kernel, out_shape=(block, block), in_specs=[pl.BlockSpec(m...]
where the time goes in v3:
time: 53.8 us; the launch traced here: 53.3 us
  Pallas kernels  51.4 us (96%)
  local copies, waits for them, and re-layouts  1.31 us (2%)
  between operations  0.64 us (1%)
    pallas_call x1, Pallas kernels, on_device(): pl.pallas_call(kernel, out_shape=(block, block), in_specs=[pl.BlockSpec(m...  51.4 us
    unnamed x2, local copies, waits for them, and re-layouts  1.31 us

profile of v3, /device:TPU:8, one launch (start us, length us, event | category | flops | bytes accessed | tf_op | source)
XLA Modules:
  0.0 53.3 jit_solution(10028737521533997846)
XLA Ops:
  0.6 51.4 %shard_map.77 = (f32[8,16,256]{2,1,0:T(8,128)S(1)}, f32[8,16,256]{2,1,0:T(8,128)S(1)}) custom-call(f32[8,16,256]{2,1,0:T(8,128)} %logk_ref.1, f32[8,16,256]{2,1,0:T(8,128)} %state_ref.1, f32[8,16,256]{2,1,0:T(8,128)} %grad_ref.1, f32[8,16,256]{2,1,0:T(8,128)} %prior_ref.1, s32[1,512]{1,0:T(1,128)} %bitcast.2, f32[1,512]{1,0:T(1,128)} %bitcast.3), custom_call_target="tpu_custom_call" | custom-call | tf_op jit(solution)/shard_map/pallas_call | solution.py:640
  52.0 0.7 %copy.10 = f32[8,16,256]{2,1,0:T(8,128)} copy(f32[8,16,256]{2,1,0:T(8,128)S(1)} %get-tuple-element.4) | data formatting | bytes 262144
  52.7 0.7 %copy.11 = f32[8,16,256]{2,1,0:T(8,128)} copy(f32[8,16,256]{2,1,0:T(8,128)S(1)} %get-tuple-element.5) | data formatting | bytes 262144

commit v4 on v3

--- a/solution.py
+++ b/solution.py
@@ -26,10 +26,10 @@
 
 def kernel(logk_ref, state_ref, grad_ref, prior_ref, cells_ref, prec_ref,
            step_ref, resid_ref,
-           lk, st, pr, src, c0, z2, vl, ystage, yrecv, ystage1, yrecv1, grad, cells_in, prec_in, r1f, wkeep,
+           lk, st, pr, src, c0, z2, wdx, ystage, yrecv, ystage1, yrecv1, grad, cells_in, prec_in, r1f, wkeep,
            kk, ca, wd, cd, sd, gg, zz, vv, cp, pp,
            c1, ca1, wd1, b1, v1, r1, p2,
-           gp, zp1, vp1, zp2, vp2, bp, v1p, gat0, gat, chunk0, chunk, cond2, ca2, wd2, rhs2, sol, weight, kc, dots, dchunk,
+           gp, zp1, vp1, zp2, vp2, bp, v1p, xp, yp, xr, yr2, cr, gat0, gat, chunk0, chunk, cond2, ca2, wd2, rhs2, sol, weight, kc, dots, dchunk,
            h_send, h_recv, g_send, g_recv, d_send, d_recv, in_sem):
     px = lax.axis_index("gx")
     py = lax.axis_index("gy")
@@ -65,9 +65,9 @@
             if dx == 0:
                 source, target = ys.at[side], yr.at[side, h:h + n]
             elif dx == 1:
-                source, target = ys.at[side, n - h:n], yr.at[side, 0:h]
+                source, target = ys.at[side, n - wx:n], yr.at[side, h - wx:h]
             else:
-                source, target = ys.at[side, 0:h], yr.at[side, h + n:h + n + h]
+                source, target = ys.at[side, 0:wx], yr.at[side, h + n:h + n + wx]
         if reverse:
             dx, dy = -dx, -dy
         return pltpu.make_async_remote_copy(
@@ -112,7 +112,7 @@
 
         def place(i):
             field[i, NY:ROWS] = jnp.concatenate([yr[0, i], yr[1, i]], axis=0)
-        loop(0, n + 2 * h, place, 4)
+        loop(h - wx, n + h + wx, place, 4)
 
     def halo_done(field, ys, yr, n, h, wx, send, recv, count=8):
         for k in range(count):
@@ -123,8 +123,96 @@
     def fine(field, slot, wx, sems):
         return (field, ystage.at[slot], yrecv.at[slot], NX, H, wx, h_send.at[sems], h_recv.at[sems])
 
-    def coarse(slot):
-        return (vl.at[slot], ystage1.at[slot], yrecv1.at[slot], NX // 2, H1, H1, h_send.at[0], h_recv.at[0])
+    send_wd = (wdx, ystage1, yrecv1, NX // 2, H1, H1, h_send.at[4], h_recv.at[4])
+
+    def pack(first, second, third):
+        r = lax.broadcasted_iota(jnp.int32, first.shape, 0) & 1
+        l = lax.broadcasted_iota(jnp.int32, first.shape, 1) & 1
+        return jnp.where(r == 0, jnp.where(l == 0, first, second), third)
+
+    def unpack(packed):
+        n = packed.shape[0]
+        r = lax.broadcasted_iota(jnp.int32, packed.shape, 0) & 1
+        l = lax.broadcasted_iota(jnp.int32, packed.shape, 1) & 1
+        even = jnp.where(r == 0, packed, pltpu.roll(packed, 1, 0))
+        return (jnp.where(l == 0, even, pltpu.roll(even, 1, 1)), jnp.where(l == 1, even, pltpu.roll(even, NZ - 1, 1)),
+                jnp.where(r == 1, packed, pltpu.roll(packed, n - 1, 0)))
+
+    def share_copy(n, k, reverse):
+        dx, dy = DIRS[k]
+        side_x, side_y = int(dx == 1), int(dy == 1)
+        if dy == 0:
+            source, target = xp.at[n, side_x], xr.at[n, 1 - side_x]
+        elif dx == 0:
+            source, target = yp.at[n, side_y], yr2.at[n, 1 - side_y]
+        else:
+            source, target = yp.at[n, side_y, side_x], cr.at[n, 1 - side_x, 1 - side_y]
+        if reverse:
+            dx, dy = -dx, -dy
+        sems = 2 * (n % 2)
+        return pltpu.make_async_remote_copy(
+            src_ref=source, dst_ref=target, send_sem=h_send.at[sems, k], recv_sem=h_recv.at[sems, k],
+            device_id={"gx": px + dx, "gy": py + dy}, device_id_type=MESH)
+
+    def share_clear():
+        for at, edge in ((0, 0), (1, PX - 1)):
+            @pl.when(px == edge)
+            def _(at=at):
+                for n in range(4):
+                    xr[n, at] = jnp.zeros((ROWS, NZ), F32)
+                    cr[n, at] = jnp.zeros((2, 8, NZ), F32)
+        for at, edge in ((0, 0), (1, PY - 1)):
+            @pl.when(py == edge)
+            def _(at=at):
+                for n in range(4):
+                    yr2[n, at] = jnp.zeros((2, 8, NZ), F32)
+                    for x in range(2):
+                        cr[n, x, at] = jnp.zeros((8, NZ), F32)
+
+    def share_send(n):
+        for half in range(2):
+            layers = [bp[1 + 3 * half + j] for j in range(3)]
+            xp[n, half] = pack(*layers)
+            yp[n, 1, half] = pack(*(jnp.where(row8 >= 4, v[8:16], v[16:24]) for v in layers))
+            yp[n, 0, half] = pack(*(jnp.where(row8 >= 4, v[16:24], v[0:8]) for v in layers))
+        for k in range(8):
+            @pl.when(exists(*DIRS[k]))
+            def _(k=k):
+                share_copy(n, k, False).start()
+
+    def share_wait(n):
+        for k in range(8):
+            @pl.when(exists(-DIRS[k][0], -DIRS[k][1]))
+            def _(k=k):
+                share_copy(n, k, True).wait_recv()
+        zero = jnp.zeros((8, NZ), F32)
+
+        def placed(v, side):
+            upper, lower = jnp.where(row8 >= 4, v, 0.0), jnp.where(row8 < 4, v, 0.0)
+            return jnp.concatenate([lower, zero, upper] if side == 0 else [zero, upper, lower], axis=0)
+        total = [bp[i] if 0 < i < RX1 - 1 else None for i in range(RX1)]
+
+        def add(i, v):
+            total[i] = v if total[i] is None else total[i] + v
+        for half, start in ((0, 1), (1, 4)):
+            for side in range(2):
+                for j, v in enumerate(unpack(yr2[n, side, half])):
+                    add(start + j, placed(v, side))
+        for side_x, start in ((0, 0), (1, 5)):
+            for j, v in enumerate(unpack(xr[n, side_x])):
+                add(start + j, v)
+            for side_y in range(2):
+                for j, v in enumerate(unpack(cr[n, side_x, side_y])):
+                    add(start + j, placed(v, side_y))
+        for i in range(RX1):
+            b1[i] = total[i]
+            v1[i] = wdx[i] * total[i]
+
+    def share_done(n):
+        for k in range(8):
+            @pl.when(exists(*DIRS[k]))
+            def _(k=k):
+                share_copy(n, k, False).wait_send()
 
     PEERS = [(dx, dy) for dy in (0, 1, -1, 2, -2) for dx in (1, 3, 2, 0) if (dx, dy) != (0, 0)]
 
@@ -263,8 +351,8 @@
     fields = [(lk, 0), (st, 1), (pr, 2), (src, 3), (z2.at[0], 4), (c0, 5), (z2.at[1], 6)]
     for field, slot in fields:
         halo_clear(field, yrecv.at[slot], NX, H)
-    for slot in range(4):
-        halo_clear(vl.at[slot], yrecv1.at[slot], NX // 2, H1)
+    halo_clear(wdx, yrecv1, NX // 2, H1)
+    share_clear()
     for field in (gp, zp1, vp1, zp2, vp2):
         def clear(i, field=field):
             field[i] = jnp.zeros((ROWS, NZ), F32)
@@ -285,7 +373,7 @@
     along = jnp.where(py > 0, 1, 0) + jnp.where(py < PY - 1, 1, 0)
     pl.semaphore_wait(barrier, (across + 1) * (along + 1) - 1)
 
-    send_prior, send_lk, send_st = fine(pr, 2, 1, 0), fine(lk, 0, H, 1), fine(st, 1, H, 2)
+    send_prior, send_lk, send_st = fine(pr, 2, 1, 0), fine(lk, 0, H, 1), fine(st, 1, 2, 2)
     halo_send(*send_prior, count=4)
     halo_send(*send_lk)
     halo_send(*send_st)
@@ -312,7 +400,7 @@
     def start_source(i):
         put(src, ystage.at[3], i + H, i, prior_row(pr, i + H) - grad[i])
     loop(0, NX, start_source, 8)
-    send_src = fine(src, 3, H, 3)
+    send_src = fine(src, 3, 2, 3)
     halo_send(*send_src)
 
     halo_wait(*send_lk)
@@ -335,7 +423,7 @@
             ca[f, i] = jnp.where(ok, a, 0.0)
             diag = a if diag is None else diag + a
         wd[i] = jnp.where(cell_inside(x), OMEGA / diag, 0.0)
-    loop(1, RX - 1, start_couplings, 14)
+    loop(2, RX - 2, start_couplings, 12)
 
     def start_level1(i):
         c1[i] = block_sum(kk[2 * i], kk[2 * i + 1], 1) * 0.125
@@ -359,6 +447,9 @@
             diag = a if diag is None else diag + a
         wd1[i] = jnp.where(cell_inside(x), OMEGA / diag, 0.0)
     loop(1, RX1 - 1, start_couplings1, 6)
+    for i in range(NX // 2):
+        put(wdx, ystage1, H1 + i, i, wd1[H1 + i, 0:NY])
+    halo_send(*send_wd)
 
     halo_wait(*send_st)
 
@@ -374,7 +465,7 @@
             cd[f, i] = jnp.where(ok, d, 0.0)
             diag = d if diag is None else diag + d
         sd[i] = diag
-    loop(1, RX - 1, start_state, 14)
+    loop(3, RX - 3, start_state, 10)
 
 
     def coarse_beside(values, d):
@@ -453,36 +544,24 @@
     def solve(source, n, reach, finish, first, after=lambda: None):
         def presmooth(i):
             vv[i] = wd[i] * source[i]
-        loop(1, RX - 1, presmooth, 14)
-
-        def restrict(i):
-            parts = []
-            for j in range(2):
-                at = 2 * i + j
-                parts.append((1.0 - OMEGA) * source[at] + coupled(ca, vv, at, vv[at], 1))
-            total = block_sum(parts[0], parts[1], 1)
-            b1[i] = total
-            v1[i] = wd1[i] * total
-        loop(1, RX1 - 1, restrict, 6)
-
-        for i in range(NX // 2):
-            put(vl.at[n], ystage1.at[n], H1 + i, i, v1[H1 + i, 0:NY])
-        send_vl = coarse(n)
-        halo_send(*send_vl)
+        loop(H - 1 - reach, H + NX + 1 + reach, presmooth, NX + 2 + 2 * reach)
+        if first:
+            halo_wait(*send_wd)
+        share_wait(n)
         if first:
             gather_cond()
             coarse_couplings()
         gather_rhs(n + 1)
         after()
         coarse_solve()
-        halo_wait(*send_vl)
         if first:
             gather_end(0, 0)
+            halo_done(*send_wd)
         gather_end(n + 1, 0)
-        halo_done(*send_vl)
+        share_done(n)
 
         for i in range(RX1):
-            v1[i] = vl[n, i] + p2[i // 2]
+            v1[i] = v1[i] + p2[i // 2]
 
         def postsmooth1(i):
             v = v1[i]
@@ -515,17 +594,18 @@
             arrive()
             gather_send(0)
         gather_send(2 * n + 1)
+        share_send(2 * n)
         if n != 0:
             arrive()
 
         def scaled(i):
             gg[i] = kk[i] * r[i]
-        loop(0, RX, scaled, 8)
+        loop(2, RX - 2, scaled, 12)
 
         def sensitivity(i):
             value = gg[i]
             zz[i] = sd[i] * value + coupled(cd, gg, i, value, 1)
-        loop(1, RX - 1, sensitivity, 14)
+        loop(3, RX - 3, sensitivity, 10)
 
         second = z2.at[n]
 
@@ -536,10 +616,11 @@
             zp2[i, 0:NY] = z
             vp2[i, 0:NY] = wd[i, 0:NY] * z
         solve(zz, 2 * n, 0, weighted, n == 0)
-        send_z2 = fine(second, 4 + 2 * n, H - 1, 1)
+        send_z2 = fine(second, 4 + 2 * n, 2, 1)
         halo_send(*send_z2)
         contribute(2 * n + 2, zp2, vp2, 1)
         gather_send(2 * n + 2)
+        share_send(2 * n + 1)
         during()
         halo_wait(*send_z2)
         halo_done(*send_z2)
@@ -574,7 +655,8 @@
     def keep_first(i, value):
         put(c0, ystage.at[5], i, i - H, value)
     hessian(src, 0, keep_first, first_products, lambda: dot_send(0), arrive_first)
-    send_c0 = fine(c0, 5, H, 1)
+    halo_done(*send_src)
+    send_c0 = fine(c0, 5, 2, 3)
     halo_send(*send_c0)
 
     def arrive_second():
@@ -612,8 +694,6 @@
         resid_ref[i] = later - beta * (curved + ratio * c)
     loop(0, NX, finish)
 
-    halo_done(*send_src)
-
 
 def scratch():
     vmem = lambda *shape: pltpu.VMEM(shape, F32)
@@ -621,16 +701,17 @@
     level1 = lambda *lead: vmem(*lead, RX1, ROWS, NZ)
     dma = pltpu.SemaphoreType.DMA
     return [
-        fine(), fine(), fine(), fine(), fine(), fine(2), level1(4),
-        vmem(7, 2, NX, H, NZ), vmem(7, 2, RX, H, NZ), vmem(4, 2, NX // 2, H, NZ), vmem(4, 2, RX1, H, NZ),
+        fine(), fine(), fine(), fine(), fine(), fine(2), level1(),
+        vmem(7, 2, NX, H, NZ), vmem(7, 2, RX, H, NZ), vmem(2, NX // 2, H, NZ), vmem(2, RX1, H, NZ),
         vmem(NX, NY, NZ), pltpu.VMEM((1, SENSORS), jnp.int32), vmem(1, SENSORS), fine(), vmem(2, NX, NY, NZ),
         fine(), fine(6), fine(), fine(6), fine(), fine(), fine(), fine(), vmem(1, 8, 128), fine(),
         level1(), level1(6), level1(), level1(), level1(), level1(), vmem(4, ROWS, NZ),
         fine(), fine(), fine(), fine(), fine(), level1(), level1(),
+        vmem(4, 2, ROWS, NZ), vmem(4, 2, 2, 8, NZ), vmem(4, 2, ROWS, NZ), vmem(4, 2, 2, 8, NZ), vmem(4, 2, 2, 8, NZ),
         vmem(WIN, PX, 2, NZ), vmem(4, WIN, PX, PIECES, 2, NZ), vmem(2, NZ), vmem(4, PIECES, 2, NZ), vmem(WIN, 8, NZ), vmem(6, WIN, 8, NZ), vmem(WIN, 8, NZ),
         vmem(WIN, 8, NZ), vmem(WIN, 8, NZ), vmem(NX, NY, NZ), vmem(NX, NY, NZ),
         vmem(2, PX * PY, 3, 128), vmem(2, 3, 128),
-        dma((4, 8)), dma((4, 8)), dma((2, WIN)), dma((3, WIN)), dma((1,)), dma((2,)), dma((6,)),
+        dma((5, 8)), dma((5, 8)), dma((2, WIN)), dma((3, WIN)), dma((1,)), dma((2,)), dma((6,)),
     ]
 
 

time: 53.8 us -> 49.1 us (0.913)
  Pallas kernels: 51.4 us -> 47 us
    pallas_call x1, Pallas kernels: 51.4 us -> 47 us  [on_device(): pl.pallas_call(kernel, out_shape=(block, block), in_specs=[pl.BlockSpec(m...]
where the time goes in v4:
time: 49.1 us; the launch traced here: 49 us
  Pallas kernels  47 us (96%)
  local copies, waits for them, and re-layouts  1.31 us (3%)
  between operations  0.64 us (1%)
    pallas_call x1, Pallas kernels, on_device(): pl.pallas_call(kernel, out_shape=(block, block), in_specs=[pl.BlockSpec(m...  47 us
    unnamed x2, local copies, waits for them, and re-layouts  1.31 us

profile of v4, /device:TPU:8, one launch (start us, length us, event | category | flops | bytes accessed | tf_op | source)
XLA Modules:
  0.0 49.0 jit_solution(10300717573989281751)
XLA Ops:
  0.6 47.0 %shard_map.77 = (f32[8,16,256]{2,1,0:T(8,128)S(1)}, f32[8,16,256]{2,1,0:T(8,128)S(1)}) custom-call(f32[8,16,256]{2,1,0:T(8,128)} %logk_ref.1, f32[8,16,256]{2,1,0:T(8,128)} %state_ref.1, f32[8,16,256]{2,1,0:T(8,128)} %grad_ref.1, f32[8,16,256]{2,1,0:T(8,128)} %prior_ref.1, s32[1,512]{1,0:T(1,128)} %bitcast.2, f32[1,512]{1,0:T(1,128)} %bitcast.3), custom_call_target="tpu_custom_call" | custom-call | tf_op jit(solution)/shard_map/pallas_call | solution.py:721
  47.7 0.7 %copy.10 = f32[8,16,256]{2,1,0:T(8,128)} copy(f32[8,16,256]{2,1,0:T(8,128)S(1)} %get-tuple-element.4) | data formatting | bytes 262144
  48.3 0.7 %copy.11 = f32[8,16,256]{2,1,0:T(8,128)} copy(f32[8,16,256]{2,1,0:T(8,128)S(1)} %get-tuple-element.5) | data formatting | bytes 262144

commit v5 on v4

--- a/solution.py
+++ b/solution.py
@@ -26,7 +26,7 @@
 
 def kernel(logk_ref, state_ref, grad_ref, prior_ref, cells_ref, prec_ref,
            step_ref, resid_ref,
-           lk, st, pr, src, c0, z2, wdx, ystage, yrecv, ystage1, yrecv1, grad, cells_in, prec_in, r1f, wkeep,
+           lk, st, pr, src, c0, z2, wdx, ystage, yrecv, ystage1, yrecv1, grad, cells_in, prec_in, r1f, wkeep, partial,
            kk, ca, wd, cd, sd, gg, zz, vv, cp, pp,
            c1, ca1, wd1, b1, v1, r1, p2,
            gp, zp1, vp1, zp2, vp2, bp, v1p, xp, yp, xr, yr2, cr, gat0, gat, chunk0, chunk, cond2, ca2, wd2, rhs2, sol, weight, kc, dots, dchunk,
@@ -214,7 +214,7 @@
             def _(k=k):
                 share_copy(n, k, False).wait_send()
 
-    PEERS = [(dx, dy) for dy in (0, 1, -1, 2, -2) for dx in (1, 3, 2, 0) if (dx, dy) != (0, 0)]
+    PEERS = [(dx, dy) for dy in (2, -2, 1, -1, 0) for dx in (2, 1, 3, 0) if (dx, dy) != (0, 0)]
 
     REACHED = (0, 1, -1, 2, -2)
 
@@ -272,7 +272,7 @@
             high = ring[d + 1] if d < WIN - 1 else zero8
             rhs2[d] = own[d] + jnp.where(y_in == 0, low, jnp.where(y_in == 3, high, 0.0))
 
-    OTHERS = [(dx, dy) for dy in range(PY) for dx in range(PX) if (dx, dy) != (0, 0)]
+    OTHERS = [(dx, dy) for dy in (4, 3, 5, 2, 6, 1, 7, 0) for dx in (2, 1, 3, 0) if (dx, dy) != (0, 0)]
 
     def dot_prepare(g, values):
         folded = [jnp.sum(v[:, 0:NZ // 2] + v[:, NZ // 2:NZ], axis=0, keepdims=True) for v in values]
@@ -551,8 +551,11 @@
         if first:
             gather_cond()
             coarse_couplings()
+        if n == 2:
+            after()
         gather_rhs(n + 1)
-        after()
+        if n == 1:
+            after()
         coarse_solve()
         if first:
             gather_end(0, 0)
@@ -578,7 +581,7 @@
             finish(i, (1.0 - OMEGA) * v + wd[i] * (source[i] + coupled(ca, vv, i, v, 1)))
         loop(H - reach, H + NX + reach, postsmooth, 10)
 
-    def hessian(r, n, keep, during, after, arrive):
+    def hessian(r, n, keep, during, after, arrive, between=lambda: None):
         def own_scaled(i):
             gp[i, 0:NY] = kk[i, 0:NY] * r[i, 0:NY]
         loop(H, H + NX, own_scaled, 8)
@@ -615,13 +618,16 @@
             put(second, ystage.at[4 + 2 * n], i, i - H, z)
             zp2[i, 0:NY] = z
             vp2[i, 0:NY] = wd[i, 0:NY] * z
-        solve(zz, 2 * n, 0, weighted, n == 0)
+        solve(zz, 2 * n, 0, weighted, n == 0, between)
         send_z2 = fine(second, 4 + 2 * n, 2, 1)
         halo_send(*send_z2)
+        if n == 1:
+            during()
         contribute(2 * n + 2, zp2, vp2, 1)
         gather_send(2 * n + 2)
         share_send(2 * n + 1)
-        during()
+        if n == 0:
+            during()
         halo_wait(*send_z2)
         halo_done(*send_z2)
 
@@ -663,7 +669,7 @@
         halo_wait(*send_c0)
         halo_done(*send_c0)
 
-    def second_products():
+    def second_start():
         rr, rc = dot_wait(0)[:2]
         alpha = rr / rc
         sums.update(rr=rr, rc=rc, alpha=alpha)
@@ -671,16 +677,24 @@
             r1f[i] = src[i] - alpha * c0[i]
         total = [zero, zero, zero]
         for i in range(NX):
-            r, w = r1f[i + H, 0:NY], wkeep[0, i] - alpha * wkeep[1, i]
+            r = r1f[i + H, 0:NY]
             total[0] = total[0] + r * r
-            total[1] = total[1] + weight[i] * w * w + r * prior_row(r1f, i + H)
+            total[1] = total[1] + r * prior_row(r1f, i + H)
             total[2] = total[2] + r * c0[i + H, 0:NY]
-        dot_prepare(1, total)
+        for j in range(3):
+            partial[j] = total[j]
+
+    def second_products():
+        weighted = zero
+        for i in range(NX):
+            w = wkeep[0, i] - sums["alpha"] * wkeep[1, i]
+            weighted = weighted + weight[i] * w * w
+        dot_prepare(1, (partial[0], partial[1] + weighted, partial[2]))
         dot_send(1)
 
     def keep_second(i, value):
         kc[i - H] = value
-    hessian(c0, 1, keep_second, second_products, lambda: None, arrive_second)
+    hessian(c0, 1, keep_second, second_products, lambda: None, arrive_second, second_start)
 
     norm, product, cross = dot_wait(1)
     alpha = sums["alpha"]
@@ -703,7 +717,7 @@
     return [
         fine(), fine(), fine(), fine(), fine(), fine(2), level1(),
         vmem(7, 2, NX, H, NZ), vmem(7, 2, RX, H, NZ), vmem(2, NX // 2, H, NZ), vmem(2, RX1, H, NZ),
-        vmem(NX, NY, NZ), pltpu.VMEM((1, SENSORS), jnp.int32), vmem(1, SENSORS), fine(), vmem(2, NX, NY, NZ),
+        vmem(NX, NY, NZ), pltpu.VMEM((1, SENSORS), jnp.int32), vmem(1, SENSORS), fine(), vmem(2, NX, NY, NZ), vmem(3, NY, NZ),
         fine(), fine(6), fine(), fine(6), fine(), fine(), fine(), fine(), vmem(1, 8, 128), fine(),
         level1(), level1(6), level1(), level1(), level1(), level1(), vmem(4, ROWS, NZ),
         fine(), fine(), fine(), fine(), fine(), level1(), level1(),

time: 49.1 us -> 46.8 us (0.953)
  Pallas kernels: 47 us -> 44.8 us
    pallas_call x1, Pallas kernels: 47 us -> 44.8 us  [on_device(): pl.pallas_call(kernel, out_shape=(block, block), in_specs=[pl.BlockSpec(m...]
where the time goes in v5:
time: 46.8 us; the launch traced here: 46.7 us
  Pallas kernels  44.8 us (96%)
  local copies, waits for them, and re-layouts  1.31 us (3%)
  between operations  0.64 us (1%)
    pallas_call x1, Pallas kernels, on_device(): pl.pallas_call(kernel, out_shape=(block, block), in_specs=[pl.BlockSpec(m...  44.8 us
    unnamed x2, local copies, waits for them, and re-layouts  1.31 us

profile of v5, /device:TPU:8, one launch (start us, length us, event | category | flops | bytes accessed | tf_op | source)
XLA Modules:
  0.0 46.7 jit_solution(15518093650641036738)
XLA Ops:
  0.6 44.8 %shard_map.77 = (f32[8,16,256]{2,1,0:T(8,128)S(1)}, f32[8,16,256]{2,1,0:T(8,128)S(1)}) custom-call(f32[8,16,256]{2,1,0:T(8,128)} %logk_ref.1, f32[8,16,256]{2,1,0:T(8,128)} %state_ref.1, f32[8,16,256]{2,1,0:T(8,128)} %grad_ref.1, f32[8,16,256]{2,1,0:T(8,128)} %prior_ref.1, s32[1,512]{1,0:T(1,128)} %bitcast.2, f32[1,512]{1,0:T(1,128)} %bitcast.3), custom_call_target="tpu_custom_call" | custom-call | tf_op jit(solution)/shard_map/pallas_call | solution.py:735
  45.4 0.7 %copy.10 = f32[8,16,256]{2,1,0:T(8,128)} copy(f32[8,16,256]{2,1,0:T(8,128)S(1)} %get-tuple-element.4) | data formatting | bytes 262144
  46.1 0.7 %copy.11 = f32[8,16,256]{2,1,0:T(8,128)} copy(f32[8,16,256]{2,1,0:T(8,128)S(1)} %get-tuple-element.5) | data formatting | bytes 262144

commit v6 on v5

--- a/solution.py
+++ b/solution.py
@@ -28,7 +28,7 @@
            step_ref, resid_ref,
            lk, st, pr, src, c0, z2, wdx, ystage, yrecv, ystage1, yrecv1, grad, cells_in, prec_in, r1f, wkeep, partial,
            kk, ca, wd, cd, sd, gg, zz, vv, cp, pp,
-           c1, ca1, wd1, b1, v1, r1, p2,
+           c1, ca1, wd1, b1, v1, p2,
            gp, zp1, vp1, zp2, vp2, bp, v1p, xp, yp, xr, yr2, cr, gat0, gat, chunk0, chunk, cond2, ca2, wd2, rhs2, sol, weight, kc, dots, dchunk,
            h_send, h_recv, g_send, g_recv, d_send, d_recv, in_sem):
     px = lax.axis_index("gx")
@@ -98,8 +98,8 @@
         ys[0, j] = value[0:H]
         ys[1, j] = value[NY - H:NY]
 
-    def halo_send(field, ys, yr, n, h, wx, send, recv, count=8):
-        for k in range(count):
+    def halo_send(field, ys, yr, n, h, wx, send, recv, count=8, first=0):
+        for k in reversed(range(first, count)):
             @pl.when(exists(*DIRS[k]))
             def _(k=k):
                 halo_copy(field, ys, yr, n, h, wx, k, send, recv, False).start()
@@ -121,9 +121,9 @@
                 halo_copy(field, ys, yr, n, h, wx, k, send, recv, False).wait_send()
 
     def fine(field, slot, wx, sems):
-        return (field, ystage.at[slot], yrecv.at[slot], NX, H, wx, h_send.at[sems], h_recv.at[sems])
-
-    send_wd = (wdx, ystage1, yrecv1, NX // 2, H1, H1, h_send.at[4], h_recv.at[4])
+        return (field, ystage.at[slot], yrecv.at[slot], NX, H, wx, h_send.at[sems % 3], h_recv.at[sems])
+
+    send_wd = (wdx, ystage1, yrecv1, NX // 2, H1, H1, h_send.at[1], h_recv.at[4])
 
     def pack(first, second, third):
         r = lax.broadcasted_iota(jnp.int32, first.shape, 0) & 1
@@ -175,7 +175,7 @@
             xp[n, half] = pack(*layers)
             yp[n, 1, half] = pack(*(jnp.where(row8 >= 4, v[8:16], v[16:24]) for v in layers))
             yp[n, 0, half] = pack(*(jnp.where(row8 >= 4, v[16:24], v[0:8]) for v in layers))
-        for k in range(8):
+        for k in reversed(range(8)):
             @pl.when(exists(*DIRS[k]))
             def _(k=k):
                 share_copy(n, k, False).start()
@@ -224,17 +224,23 @@
     def sems(g):
         return (g_send.at[0], g_recv.at[0]) if g == 0 else (g_send.at[1], g_recv.at[1 + (g - 1) % 2])
 
-    def gather_send(g):
+    def gather_send(g, which="all"):
         mine, all_ = buffers(g)
         sent, arrived = sems(g)
         for dx, dy in PEERS:
-            @pl.when((py + dy >= 0) & (py + dy < PY))
+            there = (py + dy >= 0) & (py + dy < PY)
+            if which != "all":
+                apart = px == {3: 0, 1: PX - 1}.get(dx, -1)
+                there = there & (apart if which == "apart" else jnp.logical_not(apart))
+
+            @pl.when(there)
             def _(dx=dx, dy=dy):
                 pltpu.make_async_remote_copy(
                     src_ref=mine, dst_ref=all_.at[REACH - dy, px],
                     send_sem=sent.at[REACH + dy], recv_sem=arrived.at[REACH - dy],
                     device_id={"gx": lax.rem(px + dx, PX), "gy": py + dy}, device_id_type=MESH).start()
-        all_[REACH, px] = mine[...]
+        if which != "apart":
+            all_[REACH, px] = mine[...]
 
     def gather_end(g, which):
         all_ = buffers(g)[1]
@@ -375,8 +381,10 @@
 
     send_prior, send_lk, send_st = fine(pr, 2, 1, 0), fine(lk, 0, H, 1), fine(st, 1, 2, 2)
     halo_send(*send_prior, count=4)
-    halo_send(*send_lk)
-    halo_send(*send_st)
+    halo_send(*send_lk, first=4)
+    halo_send(*send_st, first=4)
+    halo_send(*send_lk, count=4)
+    halo_send(*send_st, count=4)
 
     loads[3].wait()
     loads[4].wait()
@@ -400,6 +408,7 @@
     def start_source(i):
         put(src, ystage.at[3], i + H, i, prior_row(pr, i + H) - grad[i])
     loop(0, NX, start_source, 8)
+    halo_done(*send_prior, count=4)
     send_src = fine(src, 3, 2, 3)
     halo_send(*send_src)
 
@@ -431,6 +440,8 @@
 
     for i in range(2):
         chunk0[i:i + 1] = pick_chunk(block_sum(c1[H1 + 2 * i], c1[H1 + 2 * i + 1], 2) * 0.125)
+
+    gather_send(0, "near")
 
     inner1 = inside_yz(2)
 
@@ -449,6 +460,7 @@
     loop(1, RX1 - 1, start_couplings1, 6)
     for i in range(NX // 2):
         put(wdx, ystage1, H1 + i, i, wd1[H1 + i, 0:NY])
+    halo_done(*send_lk)
     halo_send(*send_wd)
 
     halo_wait(*send_st)
@@ -568,13 +580,11 @@
 
         def postsmooth1(i):
             v = v1[i]
-            r1[i] = (1.0 - OMEGA) * v + wd1[i] * (b1[i] + coupled(ca1, v1, i, v, 2))
+            better = (1.0 - OMEGA) * v + wd1[i] * (b1[i] + coupled(ca1, v1, i, v, 2))
+            for j in range(2):
+                if H - 1 - reach <= 2 * i + j < H + NX + 1 + reach:
+                    vv[2 * i + j] = vv[2 * i + j] + better
         loop(1, RX1 - 1, postsmooth1, 6)
-
-        def correct(i):
-            for j in range(2):
-                vv[2 * i + j] = vv[2 * i + j] + r1[i]
-        loop(1, RX1 - 1, correct)
 
         def postsmooth(i):
             v = vv[i]
@@ -595,7 +605,7 @@
         contribute(2 * n + 1, zp1, vp1, 2)
         if n == 0:
             arrive()
-            gather_send(0)
+            gather_send(0, "apart")
         gather_send(2 * n + 1)
         share_send(2 * n)
         if n != 0:
@@ -643,8 +653,7 @@
 
     def arrive_first():
         halo_wait(*send_src)
-        halo_done(*send_prior, count=4)
-        halo_done(*send_lk)
+        halo_done(*send_src)
         halo_done(*send_st)
 
     zero = jnp.zeros((NY, NZ), F32)
@@ -661,7 +670,6 @@
     def keep_first(i, value):
         put(c0, ystage.at[5], i, i - H, value)
     hessian(src, 0, keep_first, first_products, lambda: dot_send(0), arrive_first)
-    halo_done(*send_src)
     send_c0 = fine(c0, 5, 2, 3)
     halo_send(*send_c0)
 
@@ -719,13 +727,13 @@
         vmem(7, 2, NX, H, NZ), vmem(7, 2, RX, H, NZ), vmem(2, NX // 2, H, NZ), vmem(2, RX1, H, NZ),
         vmem(NX, NY, NZ), pltpu.VMEM((1, SENSORS), jnp.int32), vmem(1, SENSORS), fine(), vmem(2, NX, NY, NZ), vmem(3, NY, NZ),
         fine(), fine(6), fine(), fine(6), fine(), fine(), fine(), fine(), vmem(1, 8, 128), fine(),
-        level1(), level1(6), level1(), level1(), level1(), level1(), vmem(4, ROWS, NZ),
+        level1(), level1(6), level1(), level1(), level1(), vmem(4, ROWS, NZ),
         fine(), fine(), fine(), fine(), fine(), level1(), level1(),
         vmem(4, 2, ROWS, NZ), vmem(4, 2, 2, 8, NZ), vmem(4, 2, ROWS, NZ), vmem(4, 2, 2, 8, NZ), vmem(4, 2, 2, 8, NZ),
         vmem(WIN, PX, 2, NZ), vmem(4, WIN, PX, PIECES, 2, NZ), vmem(2, NZ), vmem(4, PIECES, 2, NZ), vmem(WIN, 8, NZ), vmem(6, WIN, 8, NZ), vmem(WIN, 8, NZ),
         vmem(WIN, 8, NZ), vmem(WIN, 8, NZ), vmem(NX, NY, NZ), vmem(NX, NY, NZ),
         vmem(2, PX * PY, 3, 128), vmem(2, 3, 128),
-        dma((5, 8)), dma((5, 8)), dma((2, WIN)), dma((3, WIN)), dma((1,)), dma((2,)), dma((6,)),
+        dma((3, 8)), dma((5, 8)), dma((2, WIN)), dma((3, WIN)), dma((1,)), dma((2,)), dma((6,)),
     ]
 
 

time: 46.8 us -> 46 us (0.983)
  Pallas kernels: 44.8 us -> 43.9 us
    pallas_call x1, Pallas kernels: 44.8 us -> 43.9 us  [on_device(): pl.pallas_call(kernel, out_shape=(block, block), in_specs=[pl.BlockSpec(m...]
where the time goes in v6:
time: 46 us; the launch traced here: 45.9 us
  Pallas kernels  43.9 us (95%)
  local copies, waits for them, and re-layouts  1.31 us (3%)
  between operations  0.64 us (1%)
    pallas_call x1, Pallas kernels, on_device(): pl.pallas_call(kernel, out_shape=(block, block), in_specs=[pl.BlockSpec(m...  43.9 us
    unnamed x2, local copies, waits for them, and re-layouts  1.31 us

profile of v6, /device:TPU:8, one launch (start us, length us, event | category | flops | bytes accessed | tf_op | source)
XLA Modules:
  0.0 45.9 jit_solution(12728681403343111564)
XLA Ops:
  0.6 43.9 %shard_map.77 = (f32[8,16,256]{2,1,0:T(8,128)S(1)}, f32[8,16,256]{2,1,0:T(8,128)S(1)}) custom-call(f32[8,16,256]{2,1,0:T(8,128)} %logk_ref.1, f32[8,16,256]{2,1,0:T(8,128)} %state_ref.1, f32[8,16,256]{2,1,0:T(8,128)} %grad_ref.1, f32[8,16,256]{2,1,0:T(8,128)} %prior_ref.1, s32[1,512]{1,0:T(1,128)} %bitcast.2, f32[1,512]{1,0:T(1,128)} %bitcast.3), custom_call_target="tpu_custom_call" | custom-call | tf_op jit(solution)/shard_map/pallas_call | solution.py:743
  44.6 0.7 %copy.10 = f32[8,16,256]{2,1,0:T(8,128)} copy(f32[8,16,256]{2,1,0:T(8,128)S(1)} %get-tuple-element.4) | data formatting | bytes 262144
  45.2 0.7 %copy.11 = f32[8,16,256]{2,1,0:T(8,128)} copy(f32[8,16,256]{2,1,0:T(8,128)S(1)} %get-tuple-element.5) | data formatting | bytes 262144
